TPU v7x, 32 devices: a whole 2x2x4 slice. The times are simulated.
32 devices in a mesh: ctx: 8 (over z, y), head: 4 (over x, core).
Axes of the slice: x: 2, y: 2, z: 4, core: 2. Of those that a mesh axis runs over, the one named last changes fastest.
Arguments:
- query_input: bfloat16 [4096, 4096], P(('ctx', 'head')), may hold values from -6 to 6
- key_input: bfloat16 [4096, 4096], P(('ctx', 'head')), may hold values from -6 to 6
- value_input: bfloat16 [4096, 4096], P(('ctx', 'head')), may hold values from -6 to 6
- cotangent: bfloat16 [4096, 4096], P(('ctx', 'head')), may hold values from -6 to 6
- level_codes: int32 [32, 13, 4096], P('head', None, 'ctx'), may hold values from 0 to 15
Outputs:
- attended: bfloat16 [4096, 4096], P(('ctx', 'head'))
- grad_queries: bfloat16 [4096, 4096], P(('ctx', 'head'))
- grad_keys: bfloat16 [4096, 4096], P(('ctx', 'head'))
- grad_values: bfloat16 [4096, 4096], P(('ctx', 'head'))
All inputs are finite; a program needn't handle non-finite values.
Results may differ from a plain program's by a relative error of at most 0.0074.
Values may be sent and summed in bfloat16 or wider, within the bound.
No kernel may reach another device: no remote copies, remote signals or barrier semaphores. Data moves between devices by JAX's collectives and lax.ppermute only.
A program may use at most 128 MiB of HBM per device.

v0:
```python
import jax
import jax.numpy as jnp
from jax import lax
from jax.sharding import PartitionSpec as P


def swapped(block, axis, stride):
    count = lax.axis_size(axis)
    route = []
    for low in range(count):
        high = low | 1 << stride
        if high != low and high < count:
            route += [(low, high), (high, low)]
    return lax.ppermute(block, axis, route)


def level_gain(level):
    if level == 0:
        return 1.0
    return 2.0 ** (-(level - 1) / 2.0)


def member_of(owner_block, member_block, bit_index):
    bit_span = 2**bit_index
    owner_set = owner_block // bit_span % 2 == 1
    member_clear = member_block // bit_span % 2 == 0
    same_parent = owner_block // (2 * bit_span) == member_block // (2 * bit_span)
    return jnp.where(owner_set & member_clear & same_parent, 1.0, 0.0).astype(jnp.float32)


def on_device(query_input, key_input, value_input, cotangent, level_codes):
    query_rows, key_rows, value_rows, cot_rows = (
        lax.all_to_all(query_input, "head", split_axis=1, concat_axis=0, tiled=True),
        lax.all_to_all(key_input, "head", split_axis=1, concat_axis=0, tiled=True),
        lax.all_to_all(value_input, "head", split_axis=1, concat_axis=0, tiled=True),
        lax.all_to_all(cotangent, "head", split_axis=1, concat_axis=0, tiled=True),
    )
    head_count = level_codes.shape[0]
    total_levels = level_codes.shape[1]
    length = query_rows.shape[0]
    head_dim = query_rows.shape[1] // head_count
    tok_bits = length.bit_length() - 1
    ctx_bits = total_levels - tok_bits - 1
    score_scale = head_dim ** (-0.5)
    head_shape = (length, head_count, head_dim)
    query_heads = query_rows.reshape(head_shape)
    key_heads = key_rows.reshape(head_shape)
    value_heads = value_rows.reshape(head_shape)
    cot_heads = cot_rows.reshape(head_shape)
    code_weights = level_codes.astype(jnp.float32) / 8.0
    my_block = lax.axis_index("ctx")
    cross_scale = jnp.stack(
        [
            code_weights[:, tok_bits + 1 + bit_index, :]
            * (score_scale * level_gain(tok_bits + 1 + bit_index))
            * (my_block // 2**bit_index % 2).astype(jnp.float32)
            for bit_index in range(ctx_bits)
        ]
    )
    row_scale = jnp.transpose(cross_scale, (0, 2, 1))
    block_state = jnp.einsum(
        "phd,phe->hde", key_heads, value_heads, preferred_element_type=jnp.float32
    )
    scaled_cot = (row_scale[..., None] * cot_heads[None]).astype(jnp.bfloat16)
    grad_state = jnp.einsum(
        "phd,bphe->bhde", query_heads, scaled_cot, preferred_element_type=jnp.float32
    )
    running = block_state
    bucket_list = []
    for bit_index in range(ctx_bits):
        partner = swapped(running, "ctx", bit_index)
        bit_set = (my_block // 2**bit_index % 2).astype(jnp.float32)
        bucket_list.append(bit_set * partner)
        running = running + partner
    bucket_sums = jnp.stack(bucket_list)
    bucket = bucket_sums.astype(jnp.bfloat16)
    term_rows = head_count * head_dim
    targets = jnp.arange(term_rows * lax.axis_size("ctx") // term_rows, dtype=jnp.int32)
    chosen = jnp.stack(
        [member_of(my_block, targets, bit_index) for bit_index in range(ctx_bits)], axis=1
    )
    spread = jnp.einsum("tb,bhde->thde", chosen, grad_state, precision=lax.Precision.HIGHEST)
    pulled = lax.psum_scatter(
        spread.reshape(term_rows * lax.axis_size("ctx"), head_dim),
        "ctx",
        scatter_dimension=0,
        tiled=True,
    ).reshape(head_count, head_dim, head_dim)
    pulled_half = pulled.astype(jnp.bfloat16)
    block_rows = min(512, length)
    steps_count = length // block_rows
    places = jnp.arange(length, dtype=jnp.int32)

    def row_step(carried_grads, block_index):
        key_grad, value_grad = carried_grads
        first_row = block_index * block_rows
        rows_at = first_row + jnp.arange(block_rows, dtype=jnp.int32)
        levels = jnp.zeros((block_rows, length), jnp.int32)
        for bit_index in range(tok_bits):
            levels = levels + (
                rows_at[:, None] // 2**bit_index != places[None, :] // 2**bit_index
            ).astype(jnp.int32)
        weight = jnp.zeros((head_count, block_rows, length), jnp.float32)
        for level_index in range(tok_bits + 1):
            weight = jnp.where(
                (levels == level_index)[None],
                code_weights[:, level_index, :, None] * level_gain(level_index),
                weight,
            )
        weight = jnp.where((places[None, :] <= rows_at[:, None])[None], weight, 0.0)
        scores = jnp.einsum(
            "phd,shd->hps", query_heads, key_heads, preferred_element_type=jnp.float32
        )
        attention = (score_scale * weight * scores).astype(jnp.bfloat16)
        local_out = jnp.einsum(
            "hps,she->phe", attention, value_heads, preferred_element_type=jnp.float32
        )
        dots = jnp.einsum(
            "phe,she->hps", cot_heads, value_heads, preferred_element_type=jnp.float32
        )
        score_grads = (score_scale * weight * dots).astype(jnp.bfloat16)
        local_qgrad = jnp.einsum(
            "hps,shd->phd", score_grads, key_heads, preferred_element_type=jnp.float32
        )
        key_grad = key_grad + jnp.einsum(
            "hps,phd->shd", score_grads, query_heads, preferred_element_type=jnp.float32
        )
        value_grad = value_grad + jnp.einsum(
            "hps,phe->she", attention, cot_heads, preferred_element_type=jnp.float32
        )
        return ((key_grad, value_grad), (local_out, local_qgrad))

    zero_grads = jnp.zeros(head_shape, jnp.float32)
    (key_local, value_local), (local_out, local_qgrad) = lax.scan(
        row_step, (zero_grads, zero_grads), jnp.arange(steps_count, dtype=jnp.int32)
    )
    local_out = local_out.reshape(head_shape)
    local_qgrad = local_qgrad.reshape(head_shape)
    cross_out = jnp.sum(
        row_scale[..., None]
        * jnp.einsum("phd,bhde->bphe", query_heads, bucket, preferred_element_type=jnp.float32),
        axis=0,
    )
    cross_qgrad = jnp.sum(
        row_scale[..., None]
        * jnp.einsum("phe,bhde->bphd", cot_heads, bucket, preferred_element_type=jnp.float32),
        axis=0,
    )
    flat_shape = (length, head_count * head_dim)
    attended = (local_out + cross_out).astype(jnp.bfloat16).reshape(flat_shape)
    grad_query = (local_qgrad + cross_qgrad).astype(jnp.bfloat16).reshape(flat_shape)
    grad_key = (
        (
            key_local
            + jnp.einsum(
                "phe,hde->phd", value_heads, pulled_half, preferred_element_type=jnp.float32
            )
        )
        .astype(jnp.bfloat16)
        .reshape(flat_shape)
    )
    grad_value = (
        (
            value_local
            + jnp.einsum("phd,hde->phe", key_heads, pulled_half, preferred_element_type=jnp.float32)
        )
        .astype(jnp.bfloat16)
        .reshape(flat_shape)
    )
    return (
        lax.all_to_all(attended, "head", split_axis=0, concat_axis=1, tiled=True),
        lax.all_to_all(grad_query, "head", split_axis=0, concat_axis=1, tiled=True),
        lax.all_to_all(grad_key, "head", split_axis=0, concat_axis=1, tiled=True),
        lax.all_to_all(grad_value, "head", split_axis=0, concat_axis=1, tiled=True),
    )


def solution(mesh):
    return jax.shard_map(
        on_device,
        mesh=mesh,
        in_specs=(
            P(("ctx", "head"), None),
            P(("ctx", "head"), None),
            P(("ctx", "head"), None),
            P(("ctx", "head"), None),
            P("head", None, "ctx"),
        ),
        out_specs=(
            P(("ctx", "head"), None),
            P(("ctx", "head"), None),
            P(("ctx", "head"), None),
            P(("ctx", "head"), None),
        ),
        check_vma=False,
    )
```

profile of v0, /device:TPU:0, one launch (start us, length us, event | category | flops | bytes accessed | tf_op | source)
XLA Modules:
  0.0 264.9 jit_solution(6928649475833172917)
XLA Ops:
  9.5 4.4 %all-to-all-start = ((bf16[128,4,1024]{2,0,1:T(8,128)(2,1)}), bf16[128,4,1024]{2,0,1:T(8,128)(2,1)S(1)}, u32[]{:S(2)}, u32[]{:S(2)}) async-start(bf16[128,4,1024]{2,0,1:T(8,128)(2,1)} %bitcast.123), calls=%async_computation | async-start | bytes 2097152 | tf_op jit(solution)/shard_map/all_to_all | solution.py:33
  15.0 13.4 %all-to-all-done = bf16[128,4,1024]{2,0,1:T(8,128)(2,1)S(1)} async-done(((bf16[128,4,1024]{2,0,1:T(8,128)(2,1)}), bf16[128,4,1024]{2,0,1:T(8,128)(2,1)S(1)}, u32[]{:S(2)}, u32[]{:S(2)}) %all-to-all-start) | async-done | bytes 1048608 | tf_op jit(solution)/shard_map/all_to_all | solution.py:33
  36.0 10.3 %all-to-all-done.4 = bf16[128,4,1024]{2,0,1:T(8,128)(2,1)S(1)} async-done(((bf16[128,4,1024]{2,0,1:T(8,128)(2,1)}), bf16[128,4,1024]{2,0,1:T(8,128)(2,1)S(1)}, u32[]{:S(2)}, u32[]{:S(2)}) %all-to-all-start.4) | async-done | bytes 1048608 | tf_op jit(solution)/shard_map/all_to_all | solution.py:36
  46.3 4.3 %all-to-all-start.1 = ((bf16[128,4,1024]{2,0,1:T(8,128)(2,1)}), bf16[128,4,1024]{2,0,1:T(8,128)(2,1)}, u32[]{:S(2)}, u32[]{:S(2)}) async-start(bf16[128,4,1024]{2,0,1:T(8,128)(2,1)} %bitcast.122), calls=%async_computation.1 | async-start | bytes 2097152 | tf_op jit(solution)/shard_map/all_to_all | solution.py:34
  53.0 4.0 %fusion.9 = f32[3,8,128,128]{2,3,0,1:T(8,128)} fusion(f32[512,8,128]{0,2,1:T(8,128)} %copy.118, f32[3,512,8]{1,0,2:T(4,128)S(1)} %copy.99, bf16[512,8,128,1]{2,1,0,3:T(8,128)(2,1)} %bitcast.136), kind=kOutput, calls=%fused_computation.19 | convolution fusion | flops 405798912 | bytes 4767744 | tf_op jit(solution)/shard_map/phd,bphe->bhde/dot_general | solution.py:65
  59.0 4.4 %fusion.53 = f32[8,8,128,128]{3,0,2,1:T(8,128)S(1)} fusion(f32[3,8,128,128]{3,0,2,1:T(4,128)S(1)} %copy.120, f32[8,1]{0,1:T(1,128)S(1)} %and_select_fusion, f32[8,1]{0,1:T(1,128)S(1)} %and_select_fusion.3, f32[8,1]{0,1:T(1,128)S(1)} %and_select_fusion.6), kind=kOutput, calls=%fused_computation.129 | convolution fusion | flops 37748784 | bytes 5767264 | tf_op jit(solution)/shard_map/tb,bhde->thde/dot_general | solution.py:82
  68.4 3.7 %all-to-all-start.2 = ((bf16[128,4,1024]{2,0,1:T(8,128)(2,1)}), bf16[128,4,1024]{2,0,1:T(8,128)(2,1)S(1)}, u32[]{:S(2)}, u32[]{:S(2)}) async-start(bf16[128,4,1024]{2,0,1:T(8,128)(2,1)} %bitcast.121), calls=%async_computation.2 | async-start | bytes 2097152 | tf_op jit(solution)/shard_map/all_to_all | solution.py:35
  73.8 12.7 %all-to-all-done.2 = bf16[128,4,1024]{2,0,1:T(8,128)(2,1)S(1)} async-done(((bf16[128,4,1024]{2,0,1:T(8,128)(2,1)}), bf16[128,4,1024]{2,0,1:T(8,128)(2,1)S(1)}, u32[]{:S(2)}, u32[]{:S(2)}) %all-to-all-start.2) | async-done | bytes 1048608 | tf_op jit(solution)/shard_map/all_to_all | solution.py:35
  94.9 14.3 %collective-permute-done = f32[8,128,128]{2,1,0:T(8,128)S(1)} collective-permute-done((f32[8,128,128]{2,1,0:T(8,128)S(1)}, f32[8,128,128]{2,1,0:T(8,128)S(1)}, u32[]{:S(2)}, u32[]{:S(2)}) %collective-permute-start) | collective-permute-done | bytes 524320 | tf_op jit(solution)/shard_map/ppermute | solution.py:14
  111.5 10.5 %multiply_convert_fusion = bf16[8,512,512]{2,1,0:T(8,128)(2,1)} fusion(f32[8,512]{1,0:T(8,128)S(1)} %get-tuple-element.53, f32[8,512]{1,0:T(8,128)S(1)} %get-tuple-element.54, f32[8,512]{1,0:T(8,128)S(1)} %copy-done.9, f32[8,512]{1,0:T(8,128)S(1)} %copy-done.10, f32[8,512]{1,0:T(8,128)S(1)} %copy-done.11, f32[8,512]{1,0:T(8,128)S(1)} %copy-done.12, ...), kind=kOutput, calls=%fused_computation | convolution fusion | flops 566231040 | bytes 9338880 | tf_op jit(solution)/shard_map/while/body/eval_jaxpr/phe,she->hps/dot_general | solution.py:118
  122.0 3.7 %collective-permute-done.1 = f32[8,128,128]{2,1,0:T(8,128)S(1)} collective-permute-done((f32[8,128,128]{2,1,0:T(8,128)S(1)}, f32[8,128,128]{2,1,0:T(8,128)S(1)}, u32[]{:S(2)}, u32[]{:S(2)}) %collective-permute-start.1) | collective-permute-done | bytes 524320 | tf_op jit(solution)/shard_map/ppermute | solution.py:14
  127.5 10.5 %multiply_convert_fusion.1 = bf16[8,512,512]{2,1,0:T(8,128)(2,1)} fusion(f32[8,512]{1,0:T(8,128)S(1)} %get-tuple-element.53, f32[8,512]{1,0:T(8,128)S(1)} %get-tuple-element.54, f32[8,512]{1,0:T(8,128)S(1)} %copy-done.9, f32[8,512]{1,0:T(8,128)S(1)} %copy-done.10, f32[8,512]{1,0:T(8,128)S(1)} %copy-done.11, f32[8,512]{1,0:T(8,128)S(1)} %copy-done.12, ...), kind=kOutput, calls=%fused_computation.1 | convolution fusion | flops 566231040 | bytes 9338880 | tf_op jit(solution)/shard_map/while/body/eval_jaxpr/phd,shd->hps/dot_general | solution.py:111
  137.9 30.2 %collective-permute-done.2 = f32[8,128,128]{2,1,0:T(8,128)S(1)} collective-permute-done((f32[8,128,128]{2,1,0:T(8,128)S(1)}, f32[8,128,128]{2,1,0:T(8,128)S(1)}, u32[]{:S(2)}, u32[]{:S(2)}) %collective-permute-start.2) | collective-permute-done | bytes 524320 | tf_op jit(solution)/shard_map/ppermute | solution.py:14
  174.1 4.1 %fusion.7 = bf16[512,8,128]{2,0,1:T(8,128)(2,1)S(1)} fusion(f32[512,8,128]{2,0,1:T(8,128)} %copy.113, bf16[8,512,512]{2,1,0:T(8,128)(2,1)} %multiply_convert_fusion, bf16[512,8,128]{2,1,0:T(8,128)(2,1)S(1)} %bitcast.130), kind=kOutput, calls=%fused_computation.16 | convolution fusion | flops 537919488 | bytes 8388608 | tf_op jit(solution)/shard_map/while/body/eval_jaxpr/hps,shd->phd/dot_general | solution.py:122
  182.1 4.5 %all-to-all-start.5 = ((bf16[4,128,1024]{2,1,0:T(8,128)(2,1)}), bf16[4,128,1024]{2,1,0:T(8,128)(2,1)}, u32[]{:S(2)}, u32[]{:S(2)}) async-start(bf16[4,128,1024]{2,1,0:T(8,128)(2,1)} %convert_element_type.558), calls=%async_computation.5 | async-start | bytes 2097152 | tf_op jit(solution)/shard_map/all_to_all | solution.py:172
  186.6 3.9 %fusion.1 = f32[512,8,128]{0,2,1:T(8,128)} fusion(f32[3,512,8]{1,0,2:T(4,128)S(1)} %copy.99, bf16[512,8,128,1]{2,1,0,3:T(8,128)(2,1)} %bitcast.137, bf16[1,8,128,128]{3,2,1,0:T(8,128)(2,1)} %copy-done.8, bf16[1,8,128,128]{3,2,1,0:T(8,128)(2,1)} %copy-done.7, bf16[1,8,128,128]{3,2,1,0:T(8,128)(2,1)S(1)} %copy-done.6), kind=kOutput, calls=%fused_computation.6 | convolution fusion | flops 406061056 | bytes 3981312 | tf_op jit(solution)/shard_map/phd,bhde->bphe/dot_general | solution.py:141
  193.4 4.1 %fusion.8 = bf16[512,8,128]{2,0,1:T(8,128)(2,1)S(1)} fusion(f32[512,8,128]{2,0,1:T(8,128)} %copy.104, bf16[8,512,512]{2,1,0:T(8,128)(2,1)} %multiply_convert_fusion.1, bf16[512,8,128]{2,1,0:T(8,128)(2,1)S(1)} %bitcast.134), kind=kOutput, calls=%fused_computation.18 | convolution fusion | flops 537919488 | bytes 8388608 | tf_op jit(solution)/shard_map/while/body/eval_jaxpr/hps,she->phe/dot_general | solution.py:115
  201.5 4.3 %all-to-all-start.3 = ((bf16[4,128,1024]{2,1,0:T(8,128)(2,1)}), bf16[4,128,1024]{2,1,0:T(8,128)(2,1)}, u32[]{:S(2)}, u32[]{:S(2)}) async-start(bf16[4,128,1024]{2,1,0:T(8,128)(2,1)} %convert_element_type.555), calls=%async_computation.3 | async-start | bytes 2097152 | tf_op jit(solution)/shard_map/all_to_all | solution.py:171
  205.8 5.2 %fusion.16 = f32[8,512,128]{2,1,0:T(8,128)} fusion(bf16[8,512,512]{2,1,0:T(8,128)(2,1)} %multiply_convert_fusion, bf16[512,8,128]{2,1,0:T(8,128)(2,1)} %bitcast.138), kind=kOutput, calls=%fused_computation.33 | convolution fusion | flops 536870912 | bytes 7340032 | tf_op jit(solution)/shard_map/while/body/eval_jaxpr/hps,phd->shd/dot_general | solution.py:125
  216.1 4.2 %all-to-all-done.3 = bf16[4,128,1024]{2,1,0:T(8,128)(2,1)} async-done(((bf16[4,128,1024]{2,1,0:T(8,128)(2,1)}), bf16[4,128,1024]{2,1,0:T(8,128)(2,1)}, u32[]{:S(2)}, u32[]{:S(2)}) %all-to-all-start.3) | async-done | bytes 1048608 | tf_op jit(solution)/shard_map/all_to_all | solution.py:171
  220.3 3.5 %all-to-all-start.6 = ((bf16[4,128,1024]{2,1,0:T(8,128)(2,1)}), bf16[4,128,1024]{2,1,0:T(8,128)(2,1)S(1)}, u32[]{:S(2)}, u32[]{:S(2)}) async-start(bf16[4,128,1024]{2,1,0:T(8,128)(2,1)} %all_to_all.118), calls=%async_computation.7 | async-start | bytes 2097152 | tf_op jit(solution)/shard_map/all_to_all | solution.py:173
  223.8 3.6 %fusion.13 = f32[8,512,128]{2,1,0:T(8,128)S(1)} fusion(bf16[8,512,512]{2,1,0:T(8,128)(2,1)} %multiply_convert_fusion.1, bf16[512,8,128]{2,1,0:T(8,128)(2,1)S(1)} %bitcast.127), kind=kOutput, calls=%fused_computation.30 | convolution fusion | flops 536870912 | bytes 7340032 | tf_op jit(solution)/shard_map/while/body/eval_jaxpr/hps,phe->she/dot_general | solution.py:128
  229.8 8.4 %all-to-all-done.6 = bf16[4,128,1024]{2,1,0:T(8,128)(2,1)S(1)} async-done(((bf16[4,128,1024]{2,1,0:T(8,128)(2,1)}), bf16[4,128,1024]{2,1,0:T(8,128)(2,1)S(1)}, u32[]{:S(2)}, u32[]{:S(2)}) %all-to-all-start.6) | async-done | bytes 1048608 | tf_op jit(solution)/shard_map/all_to_all | solution.py:173
  249.5 6.6 %all-to-all-done.7 = bf16[4,128,1024]{2,1,0:T(8,128)(2,1)S(1)} async-done(((bf16[4,128,1024]{2,1,0:T(8,128)(2,1)}), bf16[4,128,1024]{2,1,0:T(8,128)(2,1)S(1)}, u32[]{:S(2)}, u32[]{:S(2)}) %all-to-all-start.7) | async-done | bytes 1048608 | tf_op jit(solution)/shard_map/all_to_all | solution.py:174
  (93 shorter events, 71.6 us)
Async XLA Ops:
  9.5 24.1 %copy-start.3 = (bf16[128,4096]{1,0:T(8,128)(2,1)S(1)}, bf16[128,4096]{1,0:T(8,128)(2,1)}, u32[]{:S(2)}) copy-start(bf16[128,4096]{1,0:T(8,128)(2,1)} %param.6) | copy-start | bytes 3145732
  9.5 18.8 %all-to-all-start = ((bf16[128,4,1024]{2,0,1:T(8,128)(2,1)}), bf16[128,4,1024]{2,0,1:T(8,128)(2,1)S(1)}, u32[]{:S(2)}, u32[]{:S(2)}) async-start(bf16[128,4,1024]{2,0,1:T(8,128)(2,1)} %bitcast.123), calls=%async_computation | async-start | bytes 2097152 | tf_op jit(solution)/shard_map/all_to_all | solution.py:33
  28.3 17.9 %all-to-all-start.4 = ((bf16[128,4,1024]{2,0,1:T(8,128)(2,1)}), bf16[128,4,1024]{2,0,1:T(8,128)(2,1)S(1)}, u32[]{:S(2)}, u32[]{:S(2)}) async-start(bf16[128,4,1024]{2,0,1:T(8,128)(2,1)} %bitcast.120), calls=%async_computation.4 | async-start | bytes 2097152 | tf_op jit(solution)/shard_map/all_to_all | solution.py:36
  46.3 22.1 %all-to-all-start.1 = ((bf16[128,4,1024]{2,0,1:T(8,128)(2,1)}), bf16[128,4,1024]{2,0,1:T(8,128)(2,1)}, u32[]{:S(2)}, u32[]{:S(2)}) async-start(bf16[128,4,1024]{2,0,1:T(8,128)(2,1)} %bitcast.122), calls=%async_computation.1 | async-start | bytes 2097152 | tf_op jit(solution)/shard_map/all_to_all | solution.py:34
  50.5 160.5 %reduce-scatter.2.cloned.1.call-start = ((), (), s32[]{:S(2)}) async-start(), calls=%async_computation.9 | async-start | bytes 4718592 | tf_op jit(solution)/shard_map/reduce_scatter | solution.py:83
  68.4 18.0 %all-to-all-start.2 = ((bf16[128,4,1024]{2,0,1:T(8,128)(2,1)}), bf16[128,4,1024]{2,0,1:T(8,128)(2,1)S(1)}, u32[]{:S(2)}, u32[]{:S(2)}) async-start(bf16[128,4,1024]{2,0,1:T(8,128)(2,1)} %bitcast.121), calls=%async_computation.2 | async-start | bytes 2097152 | tf_op jit(solution)/shard_map/all_to_all | solution.py:35
  88.9 22.5 %copy-start.9 = (f32[8,512]{1,0:T(8,128)S(1)}, f32[8,512]{1,0:T(8,128)}, u32[]{:S(2)}) copy-start(f32[8,512]{1,0:T(8,128)} %get-tuple-element.55) | copy-start | bytes 49156
  88.9 22.5 %copy-start.10 = (f32[8,512]{1,0:T(8,128)S(1)}, f32[8,512]{1,0:T(8,128)}, u32[]{:S(2)}) copy-start(f32[8,512]{1,0:T(8,128)} %get-tuple-element.56) | copy-start | bytes 49156
  88.9 22.5 %copy-start.11 = (f32[8,512]{1,0:T(8,128)S(1)}, f32[8,512]{1,0:T(8,128)}, u32[]{:S(2)}) copy-start(f32[8,512]{1,0:T(8,128)} %get-tuple-element.57) | copy-start | bytes 49156
  88.9 22.5 %copy-start.12 = (f32[8,512]{1,0:T(8,128)S(1)}, f32[8,512]{1,0:T(8,128)}, u32[]{:S(2)}) copy-start(f32[8,512]{1,0:T(8,128)} %get-tuple-element.58) | copy-start | bytes 49156
  89.0 22.5 %copy-start.13 = (f32[8,512]{1,0:T(8,128)S(1)}, f32[8,512]{1,0:T(8,128)}, u32[]{:S(2)}) copy-start(f32[8,512]{1,0:T(8,128)} %get-tuple-element.59) | copy-start | bytes 49156
  89.0 22.5 %copy-start.14 = (f32[8,512]{1,0:T(8,128)S(1)}, f32[8,512]{1,0:T(8,128)}, u32[]{:S(2)}) copy-start(f32[8,512]{1,0:T(8,128)} %get-tuple-element.60) | copy-start | bytes 49156
  89.0 22.5 %copy-start.15 = (f32[8,512]{1,0:T(8,128)S(1)}, f32[8,512]{1,0:T(8,128)}, u32[]{:S(2)}) copy-start(f32[8,512]{1,0:T(8,128)} %get-tuple-element.61) | copy-start | bytes 49156
  89.6 19.7 %collective-permute-start = (f32[8,128,128]{2,1,0:T(8,128)S(1)}, f32[8,128,128]{2,1,0:T(8,128)S(1)}, u32[]{:S(2)}, u32[]{:S(2)}) collective-permute-start(f32[8,128,128]{2,1,0:T(8,128)S(1)} %fusion.23), channel_id=1, source_target_pairs={{0,4},{4,0},{8,12},{12,8},{16,20},{20,16},{24,28},{28,24},{1,5},{5... | collective-permute-start | bytes 1572872 | tf_op jit(solution)/shard_map/ppermute | solution.py:14
  109.4 58.8 %copy-start.5 = (bf16[1,8,128,128]{3,2,1,0:T(8,128)(2,1)}, bf16[1,8,128,128]{3,2,1,0:T(8,128)(2,1)S(1)}, u32[]{:S(2)}) copy-start(bf16[1,8,128,128]{3,2,1,0:T(8,128)(2,1)S(1)} %get-tuple-element.45) | copy-start | bytes 786436
  109.4 16.4 %collective-permute-start.1 = (f32[8,128,128]{2,1,0:T(8,128)S(1)}, f32[8,128,128]{2,1,0:T(8,128)S(1)}, u32[]{:S(2)}, u32[]{:S(2)}) collective-permute-start(f32[8,128,128]{2,1,0:T(8,128)S(1)} %get-tuple-element.46), channel_id=1, source_target_pairs={{0,8},{8,0},{4,12},{12,4},{16,24},{24,16},{20,28},{28,20},{1,9},{9... | collective-permute-start | bytes 1572872 | tf_op jit(solution)/shard_map/ppermute | solution.py:14
  111.5 16.0 %copy-start = (bf16[64,8,8,128]{3,2,1,0:T(8,128)(2,1)S(1)}, bf16[64,8,8,128]{3,2,1,0:T(8,128)(2,1)}, u32[]{:S(2)}) copy-start(bf16[64,8,8,128]{3,2,1,0:T(8,128)(2,1)} %copy.158) | copy-start | bytes 3145732
  125.8 42.4 %copy-start.7 = (bf16[1,8,128,128]{3,2,1,0:T(8,128)(2,1)}, bf16[1,8,128,128]{3,2,1,0:T(8,128)(2,1)S(1)}, u32[]{:S(2)}) copy-start(bf16[1,8,128,128]{3,2,1,0:T(8,128)(2,1)S(1)} %get-tuple-element.47) | copy-start | bytes 786436
  125.8 42.3 %collective-permute-start.2 = (f32[8,128,128]{2,1,0:T(8,128)S(1)}, f32[8,128,128]{2,1,0:T(8,128)S(1)}, u32[]{:S(2)}, u32[]{:S(2)}) collective-permute-start(f32[8,128,128]{2,1,0:T(8,128)S(1)} %get-tuple-element.48), channel_id=1, source_target_pairs={{0,16},{16,0},{4,20},{20,4},{8,24},{24,8},{12,28},{28,12},{1,17},{... | collective-permute-start | bytes 1572872 | tf_op jit(solution)/shard_map/ppermute | solution.py:14
  178.2 8.4 %copy-start.6 = (bf16[1,8,128,128]{3,2,1,0:T(8,128)(2,1)S(1)}, bf16[1,8,128,128]{3,2,1,0:T(8,128)(2,1)}, u32[]{:S(2)}) copy-start(bf16[1,8,128,128]{3,2,1,0:T(8,128)(2,1)} %copy-done.5) | copy-start | bytes 786436
  182.1 19.4 %all-to-all-start.5 = ((bf16[4,128,1024]{2,1,0:T(8,128)(2,1)}), bf16[4,128,1024]{2,1,0:T(8,128)(2,1)}, u32[]{:S(2)}, u32[]{:S(2)}) async-start(bf16[4,128,1024]{2,1,0:T(8,128)(2,1)} %convert_element_type.558), calls=%async_computation.5 | async-start | bytes 2097152 | tf_op jit(solution)/shard_map/all_to_all | solution.py:172
  201.5 18.8 %all-to-all-start.3 = ((bf16[4,128,1024]{2,1,0:T(8,128)(2,1)}), bf16[4,128,1024]{2,1,0:T(8,128)(2,1)}, u32[]{:S(2)}, u32[]{:S(2)}) async-start(bf16[4,128,1024]{2,1,0:T(8,128)(2,1)} %convert_element_type.555), calls=%async_computation.3 | async-start | bytes 2097152 | tf_op jit(solution)/shard_map/all_to_all | solution.py:171
  220.3 17.9 %all-to-all-start.6 = ((bf16[4,128,1024]{2,1,0:T(8,128)(2,1)}), bf16[4,128,1024]{2,1,0:T(8,128)(2,1)S(1)}, u32[]{:S(2)}, u32[]{:S(2)}) async-start(bf16[4,128,1024]{2,1,0:T(8,128)(2,1)} %all_to_all.118), calls=%async_computation.7 | async-start | bytes 2097152 | tf_op jit(solution)/shard_map/all_to_all | solution.py:173
  238.2 17.9 %all-to-all-start.7 = ((bf16[4,128,1024]{2,1,0:T(8,128)(2,1)}), bf16[4,128,1024]{2,1,0:T(8,128)(2,1)S(1)}, u32[]{:S(2)}, u32[]{:S(2)}) async-start(bf16[4,128,1024]{2,1,0:T(8,128)(2,1)} %all_to_all.122), calls=%async_computation.8 | async-start | bytes 2097152 | tf_op jit(solution)/shard_map/all_to_all | solution.py:174
  (4 other events, 9.7 us)
Sparse Core Ops, SparseCore 0:
  66.3 102.7 reduce-scatter.1
where the time goes:
time: 266 us; the launch traced here: 265 us
  waiting for transfers between devices  104 us (39%)
  matrix products  55.8 us (21%)
  local copies, waits for them, and re-layouts  46.9 us (18%)
  starting transfers between devices  37.6 us (14%)
  between operations  14.6 us (5%)
  other arithmetic  6.23 us (2%)
    ppermute x3, waiting for transfers between devices, swapped(): return lax.ppermute(block, axis, route)  48.2 us
    all_to_all x1, waiting for transfers between devices, on_device(): lax.all_to_all(query_input, 'head', split_axis=1, concat_axis=0, tiled=True)  13.4 us
    all_to_all x1, waiting for transfers between devices, on_device(): lax.all_to_all(value_input, 'head', split_axis=1, concat_axis=0, tiled=True)  12.7 us
    unnamed x40, local copies, waits for them, and re-layouts  12.7 us
    dot_general x1, matrix products, row_step(): jnp.einsum('phe,she->hps', cot_heads, value_heads, preferred_element_type...  10.5 us
    dot_general x1, matrix products, row_step(): jnp.einsum('phd,shd->hps', query_heads, key_heads, preferred_element_type...  10.5 us
    all_to_all x1, waiting for transfers between devices, on_device(): lax.all_to_all(cotangent, 'head', split_axis=1, concat_axis=0, tiled=True)  10.3 us
    all_to_all x1, waiting for transfers between devices, on_device(): lax.all_to_all(grad_key, 'head', split_axis=0, concat_axis=1, tiled=True)  8.37 us
  transfers between devices with their start and end apart: 12, of which 9 were waited for; matrix products, arithmetic and copies ran while one was open for 37% of the time, Pallas kernels for 0%

commit v1 on v0

v1 whole, which is shorter than its diff:
```python
import functools

import jax
import jax.numpy as jnp
from jax import lax
from jax.experimental import pallas as pl
from jax.experimental.pallas import tpu as pltpu
from jax.sharding import PartitionSpec as P


F32 = jnp.float32
BF16 = jnp.bfloat16
CHUNKS = 1
UNROLL = 4


def level_gain(level):
    if level == 0:
        return 1.0
    return 2.0 ** (-(level - 1) / 2.0)


def dot(left, right, left_dim, right_dim):
    return lax.dot_general(
        left, right, (((left_dim,), (right_dim,)), ((), ())), preferred_element_type=F32
    )


def exchanged(block, axis, mask, only=None):
    top = 1 << (mask.bit_length() - 1)
    route = [
        (index, index ^ mask)
        for index in range(lax.axis_size(axis))
        if only is None or bool(index & top) == only
    ]
    return lax.ppermute(block, axis, route)


def plus(left, right):
    return (left.astype(F32) + right.astype(F32)).astype(BF16)


def over_heads(states, side, part, step):
    count = states.shape[0]
    first = (side * CHUNKS + part) * count

    def body(index, carry):
        step(index, first + index)
        return carry

    lax.fori_loop(0, count, body, 0, unroll=min(UNROLL, count))


def lanes_of(head, dim):
    return pl.ds(pl.multiple_of(head * dim, dim), dim)


def sides(info, groups):
    for at, side in enumerate((info[0], 1 - info[0])):
        for part in range(CHUNKS):
            yield side, part, groups[at * CHUNKS + part]


def state_kernel(info, key, value, *outs, dim):
    for side, part, states in sides(info, outs):

        def step(index, head):
            lanes = lanes_of(head, dim)
            states[index] = dot(key[:, lanes], value[:, lanes], 0, 0).astype(BF16)

        over_heads(states, side, part, step)


def grad_state_kernel(info, query, cot, codes, *outs, dim, first, levels, scales):
    count = len(levels)
    for at, (side, part, _) in enumerate(sides(info, outs)):
        states = outs[at * count : (at + 1) * count]

        def step(index, head):
            lanes = lanes_of(head, dim)
            turned = query[:, lanes].T.astype(F32)
            code = codes[head].astype(F32)
            scaled = [
                (turned * (code[first + b : first + b + 1] * (scales[b] * info[1 + b].astype(F32)))).astype(BF16)
                for b in levels
            ]
            grads = dot(jnp.concatenate(scaled, axis=0), cot[:, lanes], 1, 0).astype(BF16)
            for place in range(count):
                states[place][index] = grads[place * dim : (place + 1) * dim]

        over_heads(states[0], side, part, step)


def local_kernel(query, key, value, cot, codes, out, query_grad, key_grad, value_grad, *, dim, scale):
    length = query.shape[0]
    source = lax.broadcasted_iota(jnp.int32, (length, length), 0)
    place = lax.broadcasted_iota(jnp.int32, (length, length), 1)
    apart = jnp.bitwise_xor(source, place)
    top = length.bit_length() - 1
    gains = jnp.full((length, length), scale * level_gain(top) / 8.0, F32)
    for level in range(top - 1, -1, -1):
        gains = jnp.where(apart < 2**level, scale * level_gain(level) / 8.0, gains)
    gains = jnp.where(source <= place, gains, 0.0)

    def body(head, carry):
        lanes = lanes_of(head, dim)
        q, k, v, g = query[:, lanes], key[:, lanes], value[:, lanes], cot[:, lanes]
        code = codes[head].astype(F32)
        weight = jnp.broadcast_to(code[top : top + 1], (length, length))
        for level in range(top - 1, -1, -1):
            weight = jnp.where(apart < 2**level, code[level : level + 1], weight)
        weight = weight * gains
        probs = (weight * dot(k, q, 1, 1)).astype(BF16)
        grads = (weight * dot(v, g, 1, 1)).astype(BF16)
        out[:, lanes] = dot(probs, v, 0, 0)
        query_grad[:, lanes] = dot(grads, k, 0, 0)
        key_grad[:, lanes] = dot(grads, q, 1, 0)
        value_grad[:, lanes] = dot(probs, g, 1, 0)
        return carry

    lax.fori_loop(0, codes.shape[0], body, 0, unroll=2)


def cross_terms(info, codes, head, q, g, out, query_grad, buckets, index, first, levels, scales):
    columns = codes[head].astype(F32).T
    for b, bucket in zip(levels, buckets):
        row_scale = columns[:, first + b : first + b + 1] * (scales[b] * info[1 + b].astype(F32))
        out = out + row_scale * dot(q, bucket[index], 1, 0)
        query_grad = query_grad + row_scale * dot(g, bucket[index], 1, 1)
    return out, query_grad


def cross_kernel(info, query, cot, codes, out_in, query_grad_in, *refs, dim, first, levels, scales):
    count = len(levels)
    out, query_grad = refs[-2:]
    for at, (side, part, _) in enumerate(sides(info, refs)):
        buckets = refs[at * count : (at + 1) * count]

        def step(index, head):
            lanes = lanes_of(head, dim)
            out[:, lanes], query_grad[:, lanes] = cross_terms(
                info, codes, head, query[:, lanes], cot[:, lanes], out_in[:, lanes], query_grad_in[:, lanes],
                buckets, index, first, levels, scales,
            )

        over_heads(buckets[0], side, part, step)


def last_cross_kernel(info, query, cot, codes, out_in, query_grad_in, *refs, dim, first, levels, scales):
    count = len(levels)
    out, query_grad = refs[-2:]
    for at, (side, part, _) in enumerate(sides(info, refs)):
        buckets = refs[at * count : (at + 1) * count]

        @pl.when(pl.program_id(0) == at)
        def _():
            def step(index, head):
                lanes, local = lanes_of(head, dim), lanes_of(index, dim)
                left, right = cross_terms(
                    info, codes, head, query[:, lanes], cot[:, lanes], out_in[:, lanes], query_grad_in[:, lanes],
                    buckets, index, first, levels, scales,
                )
                out[:, local] = left.astype(BF16)
                query_grad[:, local] = right.astype(BF16)

            over_heads(buckets[0], side, part, step)


def pull_kernel(info, key, value, key_grad_in, value_grad_in, *refs, dim):
    key_grad, value_grad = refs[-2:]
    for at, (side, part, _) in enumerate(sides(info, refs)):
        pull, near = refs[2 * at : 2 * at + 2]

        @pl.when(pl.program_id(0) == at)
        def _():
            def step(index, head):
                lanes, local = lanes_of(head, dim), lanes_of(index, dim)
                pulled = plus(pull[index], near[index])
                key_grad[:, local] = (key_grad_in[:, lanes] + dot(value[:, lanes], pulled, 1, 1)).astype(BF16)
                value_grad[:, local] = (value_grad_in[:, lanes] + dot(key[:, lanes], pulled, 1, 0)).astype(BF16)

            over_heads(pull, side, part, step)


def on_device(query, key, value, cot, level_codes):
    length, width = query.shape
    shard_heads, total_levels, _ = level_codes.shape
    head_count, ctx_count = lax.axis_size("head"), lax.axis_size("ctx")
    heads = shard_heads * head_count
    dim = width // heads
    part_heads = heads // (2 * CHUNKS)
    tok_bits = length.bit_length() - 1
    head_bits = head_count.bit_length() - 1
    cross = total_levels - tok_bits - 1
    first = tok_bits + 1
    scale = dim**-0.5
    scales = tuple(scale * level_gain(first + b) / 8.0 for b in range(cross))
    hops = [("head", 2 << bit) for bit in range(head_bits - 1)]
    ctx_bits = ctx_count.bit_length() - 1
    for bit in range(ctx_bits):
        hops.append(("ctx", 3 << (bit - 1) if bit and bit == ctx_bits - 1 else 1 << bit))
    my_head = lax.axis_index("head")
    mine = lax.axis_index("ctx") * head_count + my_head
    bits = [mine // 2**b % 2 for b in range(cross)]
    info = jnp.stack([bits[0], *bits]).astype(jnp.int32)

    padded = -(-total_levels // 16) * 16
    codes = jnp.pad(level_codes.astype(BF16), ((0, 0), (0, padded - total_levels), (0, 0)))
    codes = codes.reshape(shard_heads, padded, head_count, length).transpose(2, 0, 1, 3)
    got = [lax.dynamic_index_in_dim(codes, my_head, keepdims=False)]
    for mask in range(1, head_count):
        got.append(exchanged(lax.dynamic_index_in_dim(codes, my_head ^ mask, keepdims=False), "head", mask))
    groups = []
    for group in range(head_count):
        chosen = got[0]
        for mask in range(1, head_count):
            chosen = jnp.where(my_head ^ group == mask, got[mask], chosen)
        groups.append(chosen)
    codes = jnp.concatenate(groups, axis=0)

    in_smem, in_vmem = pl.BlockSpec(memory_space=pltpu.SMEM), pl.BlockSpec(memory_space=pltpu.VMEM)
    state_out = pltpu.VMEM((part_heads, dim, dim), BF16)
    wide = pltpu.VMEM((length, width), F32)
    narrow = jax.ShapeDtypeStruct((length, width), BF16)

    def run(body, args, outs, work, **grid):
        args = [arg if arg is info else pltpu.with_memory_space_constraint(arg, pltpu.VMEM) for arg in args]
        return pl.pallas_call(
            body,
            in_specs=[in_smem if arg is info else in_vmem for arg in args],
            out_shape=outs,
            cost_estimate=pl.CostEstimate(
                flops=work * heads * length * dim * dim * 2, bytes_accessed=0, transcendentals=0
            ),
            compiler_params=pltpu.CompilerParams(vmem_limit_bytes=12 << 20),
            **(grid or dict(out_specs=[in_vmem] * len(outs))),
        )(*args)

    states = run(functools.partial(state_kernel, dim=dim), [info, key, value], [state_out] * (2 * CHUNKS), 1)
    own, other = states[:CHUNKS], states[CHUNKS:]

    def grad_states(levels):
        count = len(levels)
        flat = run(
            functools.partial(grad_state_kernel, dim=dim, first=first, levels=levels, scales=scales),
            [info, query, cot, codes],
            [state_out] * (2 * CHUNKS * count),
            count,
        )
        for place, b in enumerate(levels):
            grads[b] = [flat[part * count + place] for part in range(2 * CHUNKS)]

    grads = {}
    grad_states((cross - 1,))
    grad_states(tuple(range(cross - 1)))

    parts = range(CHUNKS)
    arrived = [exchanged(other[part], "head", 1) for part in parts]
    buckets = [arrived + [exchanged(own[part], "head", 1, False) for part in parts]]
    running = [plus(own[part], arrived[part]) for part in parts]
    for at, (axis, mask) in enumerate(hops):
        top = at == len(hops) - 1
        arrived = [exchanged(running[part], axis, mask, False if top else None) for part in parts]
        buckets.append(arrived + [exchanged(arrived[part], "head", 1) for part in parts])
        if not top:
            running = [plus(running[part], arrived[part]) for part in parts]

    near = [exchanged(grads[0][CHUNKS + part], "head", 1, True) for part in parts]
    near += [exchanged(grads[0][part], "head", 1, True) for part in parts]
    pulled = [None] * CHUNKS
    for at in range(len(hops) - 1, -1, -1):
        axis, mask = hops[at]
        for part in parts:
            grad = plus(grads[at + 1][part], exchanged(grads[at + 1][CHUNKS + part], "head", 1))
            if pulled[part] is None:
                pulled[part] = exchanged(grad, axis, mask, True)
            else:
                pulled[part] = plus(pulled[part], exchanged(plus(pulled[part], grad), axis, mask))
    pulled += [exchanged(pulled[part], "head", 1) for part in parts]

    out, query_grad, key_grad, value_grad = run(
        functools.partial(local_kernel, dim=dim, scale=scale), [query, key, value, cot, codes], [wide] * 4, 6
    )

    def crossed(body, levels, outs, **grid):
        refs = [buckets[b][part] for part in range(2 * CHUNKS) for b in levels]
        return run(
            functools.partial(body, dim=dim, first=first, levels=levels, scales=scales),
            [info, query, cot, codes, out, query_grad, *refs],
            outs,
            2 * len(levels),
            **grid,
        )

    def block_at(step, core_head):
        side = jnp.where(step < CHUNKS, core_head, 1 - core_head)
        return side * CHUNKS + step % CHUNKS

    def last_grid():
        spec = pl.BlockSpec((length, part_heads * dim), lambda step: (0, block_at(step, lax.axis_index("head") % 2)))
        return dict(grid=(2 * CHUNKS,), out_specs=[spec] * 2)

    split = cross - 1
    out, query_grad = crossed(cross_kernel, tuple(range(split)), [wide] * 2)
    attended, query_grad = crossed(last_cross_kernel, tuple(range(split, cross)), [narrow] * 2, **last_grid())
    refs = [piece for part in range(2 * CHUNKS) for piece in (pulled[part], near[part])]
    key_grad, value_grad = run(
        functools.partial(pull_kernel, dim=dim),
        [info, key, value, key_grad, value_grad, *refs],
        [narrow] * 2,
        2,
        **last_grid(),
    )
    return attended, query_grad, key_grad, value_grad


def solution(mesh):
    rows = P(("ctx", "head"), None)
    return jax.shard_map(
        on_device,
        mesh=mesh,
        in_specs=(rows, rows, rows, rows, P("head", None, "ctx")),
        out_specs=(rows, rows, rows, rows),
        check_vma=False,
    )
```

time: 266 us -> 124 us (0.47)
  the two profiles are of different devices: /device:TPU:0 before, /device:TPU:17 now
where the time goes in v1:
time: 124 us; the launch traced here: 123 us
  waiting for transfers between devices  58.8 us (47%)
  Pallas kernels  33.9 us (27%)
  starting transfers between devices  23.8 us (19%)
  other arithmetic  3.15 us (3%)
  local copies, waits for them, and re-layouts  2.62 us (2%)
    ppermute x24, waiting for transfers between devices, exchanged(): return lax.ppermute(block, axis, route)  58.8 us
    pallas_call x7, Pallas kernels, run(): pl.pallas_call(body, in_specs=[in_smem if arg is info else in_vmem for ar...  33.9 us
    ppermute x24, starting transfers between devices, exchanged(): return lax.ppermute(block, axis, route)  23.8 us
    unnamed x15, local copies, waits for them, and re-layouts  2.49 us
  transfers between devices with their start and end apart: 24, of which 5 were waited for; matrix products, arithmetic and copies ran while one was open for 2% of the time, Pallas kernels for 25%

profile of v1, /device:TPU:17, one launch (start us, length us, event | category | flops | bytes accessed | tf_op | source)
XLA Modules:
  0.0 123.3 jit_solution(9729934288879402883)
XLA Ops:
  1.9 1.8 %collective-permute-start = (bf16[8,16,128]{2,1,0:T(8,128)(2,1)S(1)}, bf16[8,16,128]{2,1,0:T(8,128)(2,1)S(1)}, u32[]{:S(2)}, u32[]{:S(2)}) collective-permute-start(bf16[8,16,128]{2,1,0:T(8,128)(2,1)S(1)} %bitcast.26), channel_id=1, source_target_pairs={{0,3},{1,2},{2,1},{3,0},{4,7},{5,6},{6,5},{7,4},{8,11},{9,10},{10,... | collective-permute-start | bytes 98312 | tf_op jit(solution)/shard_map/ppermute | solution.py:36
  6.7 3.1 %shard_map.85 = (bf16[16,128,128]{2,1,0:T(8,128)(2,1)S(1)}, bf16[16,128,128]{2,1,0:T(8,128)(2,1)}) custom-call(s32[6]{0:T(128)S(1)} %stack.24.info, bf16[128,4096]{1,0:T(8,128)(2,1)S(1)} %copy-done.2, bf16[128,4096]{1,0:T(8,128)(2,1)S(1)} %copy-done.4), custom_call_target="tpu_custom_call" | custom-call | flops 134217728 | tf_op jit(solution)/shard_map/pallas_call | solution.py:228
  10.2 2.4 %shard_map.88 = (bf16[16,128,128]{2,1,0:T(8,128)(2,1)S(1)}, bf16[16,128,128]{2,1,0:T(8,128)(2,1)S(1)}) custom-call(s32[6]{0:T(128)S(1)} %stack.24.info, bf16[128,4096]{1,0:T(8,128)(2,1)S(1)} %copy-done, bf16[128,4096]{1,0:T(8,128)(2,1)S(1)} %copy-done.1, bf16[32,16,128]{2,1,0:T(8,128)(2,1)S(1)} %pad_maximum_fusion.codes), custom_call_target="tpu_custom_call" | custom-call | flops 134217728 | tf_op jit(solution)/shard_map/pallas_call | solution.py:228
  12.9 3.2 %shard_map.89 = (bf16[16,128,128]{2,1,0:T(8,128)(2,1)S(1)}, bf16[16,128,128]{2,1,0:T(8,128)(2,1)S(1)}, bf16[16,128,128]{2,1,0:T(8,128)(2,1)S(1)}, bf16[16,128,12...) custom-call(s32[6]{0:T(128)S(1)} %stack.24.info, ...), custom_call_target="tpu_custom_call" | custom-call | flops 536870912 | tf_op jit(solution)/shard_map/pallas_call | solution.py:228
  18.1 2.1 %collective-permute-start.14 = (bf16[16,128,128]{2,1,0:T(8,128)(2,1)S(1)}, bf16[16,128,128]{2,1,0:T(8,128)(2,1)S(1)}, u32[]{:S(2)}, u32[]{:S(2)}) collective-permute-start(bf16[16,128,128]{2,1,0:T(8,128)(2,1)S(1)} %add_convert_fusion.3), channel_id=1, source_target_pairs={{16,8},{20,12},{24,0},{28,4},{17,9},{21,13},{25,1},{29,5},{18,10},... | collective-permute-start | bytes 1572872 | tf_op jit(solution)/shard_map/ppermute | solution.py:36
  21.0 9.1 %collective-permute-done.4.refs_1_ = bf16[16,128,128]{2,1,0:T(8,128)(2,1)S(1)} collective-permute-done((bf16[16,128,128]{2,1,0:T(8,128)(2,1)S(1)}, bf16[16,128,128]{2,1,0:T(8,128)(2,1)S(1)}, u32[]{:S(2)}, u32[]{:S(2)}) %collective-permute-start.4) | collective-permute-done | bytes 524320 | tf_op jit(solution)/shard_map/ppermute | solution.py:36
  30.2 1.3 %collective-permute-start.5 = (bf16[16,128,128]{2,1,0:T(8,128)(2,1)S(1)}, bf16[16,128,128]{2,1,0:T(8,128)(2,1)S(1)}, u32[]{:S(2)}, u32[]{:S(2)}) collective-permute-start(bf16[16,128,128]{2,1,0:T(8,128)(2,1)S(1)} %add_convert_fusion.6), channel_id=1, source_target_pairs={{0,4},{4,0},{8,12},{12,8},{16,20},{20,16},{24,28},{28,24},{1,5},{5... | collective-permute-start | bytes 1572872 | tf_op jit(solution)/shard_map/ppermute | solution.py:36
  31.5 10.8 %collective-permute-done.14 = bf16[16,128,128]{2,1,0:T(8,128)(2,1)S(1)} collective-permute-done((bf16[16,128,128]{2,1,0:T(8,128)(2,1)S(1)}, bf16[16,128,128]{2,1,0:T(8,128)(2,1)S(1)}, u32[]{:S(2)}, u32[]{:S(2)}) %collective-permute-start.14) | collective-permute-done | bytes 524320 | tf_op jit(solution)/shard_map/ppermute | solution.py:36
  42.6 1.3 %collective-permute-start.19 = (bf16[16,128,128]{2,1,0:T(8,128)(2,1)S(1)}, bf16[16,128,128]{2,1,0:T(8,128)(2,1)S(1)}, u32[]{:S(2)}, u32[]{:S(2)}) collective-permute-start(bf16[16,128,128]{2,1,0:T(8,128)(2,1)S(1)} %get-tuple-element.43), channel_id=1, source_target_pairs={{0,1},{1,0},{2,3},{3,2},{4,5},{5,4},{6,7},{7,6},{8,9},{9,8},{10,11... | collective-permute-start | bytes 1572872 | tf_op jit(solution)/shard_map/ppermute | solution.py:36
  44.1 1.7 %collective-permute-start.6 = (bf16[16,128,128]{2,1,0:T(8,128)(2,1)S(1)}, bf16[16,128,128]{2,1,0:T(8,128)(2,1)S(1)}, u32[]{:S(2)}, u32[]{:S(2)}) collective-permute-start(bf16[16,128,128]{2,1,0:T(8,128)(2,1)S(1)} %add_convert_fusion.5), channel_id=1, source_target_pairs={{0,8},{4,12},{8,0},{12,4},{16,24},{20,28},{24,16},{28,20},{1,9},{5... | collective-permute-start | bytes 1572872 | tf_op jit(solution)/shard_map/ppermute | solution.py:36
  45.8 9.0 %collective-permute-done.16 = bf16[16,128,128]{2,1,0:T(8,128)(2,1)S(1)} collective-permute-done((bf16[16,128,128]{2,1,0:T(8,128)(2,1)S(1)}, bf16[16,128,128]{2,1,0:T(8,128)(2,1)S(1)}, u32[]{:S(2)}, u32[]{:S(2)}) %collective-permute-start.16) | collective-permute-done | bytes 524320 | tf_op jit(solution)/shard_map/ppermute | solution.py:36
  55.2 1.3 %collective-permute-start.18 = (bf16[16,128,128]{2,1,0:T(8,128)(2,1)S(1)}, bf16[16,128,128]{2,1,0:T(8,128)(2,1)S(1)}, u32[]{:S(2)}, u32[]{:S(2)}) collective-permute-start(bf16[16,128,128]{2,1,0:T(8,128)(2,1)S(1)} %fusion.2), channel_id=1, source_target_pairs={{0,4},{4,0},{8,12},{12,8},{16,20},{20,16},{24,28},{28,24},{1,5},{5... | collective-permute-start | bytes 1572872 | tf_op jit(solution)/shard_map/ppermute | solution.py:36
  56.5 9.6 %collective-permute-done.6.refs_3_ = bf16[16,128,128]{2,1,0:T(8,128)(2,1)S(1)} collective-permute-done((bf16[16,128,128]{2,1,0:T(8,128)(2,1)S(1)}, bf16[16,128,128]{2,1,0:T(8,128)(2,1)S(1)}, u32[]{:S(2)}, u32[]{:S(2)}) %collective-permute-start.6) | collective-permute-done | bytes 524320 | tf_op jit(solution)/shard_map/ppermute | solution.py:36
  66.2 1.3 %collective-permute-start.11 = (bf16[16,128,128]{2,1,0:T(8,128)(2,1)S(1)}, bf16[16,128,128]{2,1,0:T(8,128)(2,1)S(1)}, u32[]{:S(2)}, u32[]{:S(2)}) collective-permute-start(bf16[16,128,128]{2,1,0:T(8,128)(2,1)S(1)} %add_convert_fusion.4), channel_id=1, source_target_pairs={{0,24},{4,28},{8,16},{12,20},{1,25},{5,29},{9,17},{13,21},{2,26},{... | collective-permute-start | bytes 1572872 | tf_op jit(solution)/shard_map/ppermute | solution.py:36
  68.6 1.4 %collective-permute-start.7 = (bf16[16,128,128]{2,1,0:T(8,128)(2,1)S(1)}, bf16[16,128,128]{2,1,0:T(8,128)(2,1)S(1)}, u32[]{:S(2)}, u32[]{:S(2)}) collective-permute-start(bf16[16,128,128]{2,1,0:T(8,128)(2,1)S(1)} %get-tuple-element.29), channel_id=1, source_target_pairs={{0,1},{2,3},{4,5},{6,7},{8,9},{10,11},{12,13},{14,15},{16,17},{18,... | collective-permute-start | bytes 1572872 | tf_op jit(solution)/shard_map/ppermute | solution.py:36
  70.0 2.3 %collective-permute-start.8 = (bf16[16,128,128]{2,1,0:T(8,128)(2,1)S(1)}, bf16[16,128,128]{2,1,0:T(8,128)(2,1)S(1)}, u32[]{:S(2)}, u32[]{:S(2)}) collective-permute-start(bf16[16,128,128]{2,1,0:T(8,128)(2,1)S(1)} %collective-permute-done.4.refs_1_), channel_id=1, source_target_pairs={{0,1},{1,0},{2,3},{3,2},{4,5},{5,4},{6,7},{7,6},{8,9},{9,8},{10,11... | collective-permute-start | bytes 1572872 | tf_op jit(solution)/shard_map/ppermute | solution.py:36
  72.4 20.2 %collective-permute-done.11.refs_0_ = bf16[16,128,128]{2,1,0:T(8,128)(2,1)S(1)} collective-permute-done((bf16[16,128,128]{2,1,0:T(8,128)(2,1)S(1)}, bf16[16,128,128]{2,1,0:T(8,128)(2,1)S(1)}, u32[]{:S(2)}, u32[]{:S(2)}) %collective-permute-start.11) | collective-permute-done | bytes 524320 | tf_op jit(solution)/shard_map/ppermute | solution.py:36
  92.5 1.3 %collective-permute-start.10 = (bf16[16,128,128]{2,1,0:T(8,128)(2,1)S(1)}, bf16[16,128,128]{2,1,0:T(8,128)(2,1)S(1)}, u32[]{:S(2)}, u32[]{:S(2)}) collective-permute-start(bf16[16,128,128]{2,1,0:T(8,128)(2,1)S(1)} %collective-permute-done.6.refs_3_), channel_id=1, source_target_pairs={{0,1},{1,0},{2,3},{3,2},{4,5},{5,4},{6,7},{7,6},{8,9},{9,8},{10,11... | collective-permute-start | bytes 1572872 | tf_op jit(solution)/shard_map/ppermute | solution.py:36
  94.2 2.4 %collective-permute-start.21 = (bf16[16,128,128]{2,1,0:T(8,128)(2,1)S(1)}, bf16[16,128,128]{2,1,0:T(8,128)(2,1)S(1)}, u32[]{:S(2)}, u32[]{:S(2)}) collective-permute-start(bf16[16,128,128]{2,1,0:T(8,128)(2,1)S(1)} %get-tuple-element.44), channel_id=1, source_target_pairs={{1,0},{3,2},{5,4},{7,6},{9,8},{11,10},{13,12},{15,14},{17,16},{19,... | collective-permute-start | bytes 1572872 | tf_op jit(solution)/shard_map/ppermute | solution.py:36
  96.6 1.3 %collective-permute-start.23 = (bf16[16,128,128]{2,1,0:T(8,128)(2,1)S(1)}, bf16[16,128,128]{2,1,0:T(8,128)(2,1)S(1)}, u32[]{:S(2)}, u32[]{:S(2)}) collective-permute-start(bf16[16,128,128]{2,1,0:T(8,128)(2,1)S(1)} %get-tuple-element.45), channel_id=1, source_target_pairs={{1,0},{3,2},{5,4},{7,6},{9,8},{11,10},{13,12},{15,14},{17,16},{19,... | collective-permute-start | bytes 1572872 | tf_op jit(solution)/shard_map/ppermute | solution.py:36
  98.1 10.3 %shard_map.84 = (f32[128,4096]{1,0:T(8,128)S(1)}, f32[128,4096]{1,0:T(8,128)S(1)}, f32[128,4096]{1,0:T(8,128)S(1)}, f32[128,4096]{1,0:T(8,128)S(1)}) custom-call(bf16[128,4096]{1,0:T(8,128)(2,1)S(1)} %copy-done, bf16[128,4096]{1,0:T(8,128)(2,1)S(1)} %copy-done.3, bf16[128,4096]{1,0:T(8,128)(2,1)S(1)} %copy-done.5, bf16[128,4096]{1,0:T(8,128)(2,1)S(1)} %copy-done.1, ...), custom_call_target="tpu_custom_call" | custom-call | flops 805306368 | tf_op jit(solution)/shard_map/pallas_call | solution.py:228
  108.4 6.7 %shard_map.86 = (f32[128,4096]{1,0:T(8,128)S(1)}, f32[128,4096]{1,0:T(8,128)S(1)}) custom-call(s32[6]{0:T(128)S(1)} %stack.24.info, bf16[128,4096]{1,0:T(8,128)(2,1)S(1)} %copy-done, bf16[128,4096]{1,0:T(8,128)(2,1)S(1)} %copy-done.1, bf16[32,16,128]{2,1,0:T(8,128)(2,1)S(1)} %pad_maximum_fusion.codes, f32[128,4096]{1,0:T(8,128)S(1)} %get-tuple-element.26.out_in, ...), custom_call_target="tpu_custom_call" | custom-call | flops 1073741824 | tf_op jit(solution)/shard_map/pallas_call | solution.py:228
  115.1 4.5 %shard_map.87 = (bf16[128,4096]{1,0:T(8,128)(2,1)}, bf16[128,4096]{1,0:T(8,128)(2,1)}) custom-call(s32[6]{0:T(128)S(1)} %stack.24.info, bf16[128,4096]{1,0:T(8,128)(2,1)S(1)} %copy-done, bf16[128,4096]{1,0:T(8,128)(2,1)S(1)} %copy-done.1, bf16[32,16,128]{2,1,0:T(8,128)(2,1)S(1)} %pad_maximum_fusion.codes, f32[128,4096]{1,0:T(8,128)S(1)} %get-tuple-element.30.out_in, ...), custom_call_target="tpu_custom_call" | custom-call | flops 268435456 | tf_op jit(solution)/shard_map/pallas_call | solution.py:228
  119.6 3.7 %shard_map.90 = (bf16[128,4096]{1,0:T(8,128)(2,1)}, bf16[128,4096]{1,0:T(8,128)(2,1)}) custom-call(s32[6]{0:T(128)S(1)} %stack.24.info, bf16[128,4096]{1,0:T(8,128)(2,1)S(1)} %copy-done.3, bf16[128,4096]{1,0:T(8,128)(2,1)S(1)} %copy-done.5, f32[128,4096]{1,0:T(8,128)S(1)} %get-tuple-element.34.key_grad_in, f32[128,4096]{1,0:T(8,128)S(1)} %get-tuple-element.35.value_grad_in, ...), custom_call_target="tpu_custom_call" | custom-call | flops 268435456 | tf_op jit(solution)/shard_map/pallas_call | solution.py:228
  (61 shorter events, 10.0 us)
Async XLA Ops:
  1.9 8.3 %collective-permute-start = (bf16[8,16,128]{2,1,0:T(8,128)(2,1)S(1)}, bf16[8,16,128]{2,1,0:T(8,128)(2,1)S(1)}, u32[]{:S(2)}, u32[]{:S(2)}) collective-permute-start(bf16[8,16,128]{2,1,0:T(8,128)(2,1)S(1)} %bitcast.26), channel_id=1, source_target_pairs={{0,3},{1,2},{2,1},{3,0},{4,7},{5,6},{6,5},{7,4},{8,11},{9,10},{10,... | collective-permute-start | bytes 98312 | tf_op jit(solution)/shard_map/ppermute | solution.py:36
  3.7 6.4 %collective-permute-start.1 = (bf16[8,16,128]{2,1,0:T(8,128)(2,1)S(1)}, bf16[8,16,128]{2,1,0:T(8,128)(2,1)S(1)}, u32[]{:S(2)}, u32[]{:S(2)}) collective-permute-start(bf16[8,16,128]{2,1,0:T(8,128)(2,1)S(1)} %bitcast.27), channel_id=1, source_target_pairs={{0,2},{1,3},{2,0},{3,1},{4,6},{5,7},{6,4},{7,5},{8,10},{9,11},{10,... | collective-permute-start | bytes 98312 | tf_op jit(solution)/shard_map/ppermute | solution.py:36
  4.0 6.2 %collective-permute-start.2 = (bf16[8,16,128]{2,1,0:T(8,128)(2,1)S(1)}, bf16[8,16,128]{2,1,0:T(8,128)(2,1)S(1)}, u32[]{:S(2)}, u32[]{:S(2)}) collective-permute-start(bf16[8,16,128]{2,1,0:T(8,128)(2,1)S(1)} %bitcast.28), channel_id=1, source_target_pairs={{0,1},{1,0},{2,3},{3,2},{4,5},{5,4},{6,7},{7,6},{8,9},{9,8},{10,11... | collective-permute-start | bytes 98312 | tf_op jit(solution)/shard_map/ppermute | solution.py:36
  9.9 6.7 %collective-permute-start.3 = (bf16[16,128,128]{2,1,0:T(8,128)(2,1)}, bf16[16,128,128]{2,1,0:T(8,128)(2,1)S(1)}, u32[]{:S(2)}, u32[]{:S(2)}) collective-permute-start(bf16[16,128,128]{2,1,0:T(8,128)(2,1)} %get-tuple-element.28), channel_id=1, source_target_pairs={{0,1},{1,0},{2,3},{3,2},{4,5},{5,4},{6,7},{7,6},{8,9},{9,8},{10,11... | collective-permute-start | bytes 1572872 | tf_op jit(solution)/shard_map/ppermute | solution.py:36
  12.7 5.3 %collective-permute-start.13 = (bf16[16,128,128]{2,1,0:T(8,128)(2,1)S(1)}, bf16[16,128,128]{2,1,0:T(8,128)(2,1)S(1)}, u32[]{:S(2)}, u32[]{:S(2)}) collective-permute-start(bf16[16,128,128]{2,1,0:T(8,128)(2,1)S(1)} %get-tuple-element.37), channel_id=1, source_target_pairs={{0,1},{1,0},{2,3},{3,2},{4,5},{5,4},{6,7},{7,6},{8,9},{9,8},{10,11... | collective-permute-start | bytes 1572872 | tf_op jit(solution)/shard_map/ppermute | solution.py:36
  16.2 15.3 %collective-permute-start.15 = (bf16[16,128,128]{2,1,0:T(8,128)(2,1)S(1)}, bf16[16,128,128]{2,1,0:T(8,128)(2,1)S(1)}, u32[]{:S(2)}, u32[]{:S(2)}) collective-permute-start(bf16[16,128,128]{2,1,0:T(8,128)(2,1)S(1)} %get-tuple-element.39), channel_id=1, source_target_pairs={{0,1},{1,0},{2,3},{3,2},{4,5},{5,4},{6,7},{7,6},{8,9},{9,8},{10,11... | collective-permute-start | bytes 1572872 | tf_op jit(solution)/shard_map/ppermute | solution.py:36
  16.7 13.3 %collective-permute-start.4 = (bf16[16,128,128]{2,1,0:T(8,128)(2,1)S(1)}, bf16[16,128,128]{2,1,0:T(8,128)(2,1)S(1)}, u32[]{:S(2)}, u32[]{:S(2)}) collective-permute-start(bf16[16,128,128]{2,1,0:T(8,128)(2,1)S(1)} %add_convert_fusion.7), channel_id=1, source_target_pairs={{0,2},{1,3},{2,0},{3,1},{4,6},{5,7},{6,4},{7,5},{8,10},{9,11},{10,... | collective-permute-start | bytes 1572872 | tf_op jit(solution)/shard_map/ppermute | solution.py:36
  18.1 24.2 %collective-permute-start.14 = (bf16[16,128,128]{2,1,0:T(8,128)(2,1)S(1)}, bf16[16,128,128]{2,1,0:T(8,128)(2,1)S(1)}, u32[]{:S(2)}, u32[]{:S(2)}) collective-permute-start(bf16[16,128,128]{2,1,0:T(8,128)(2,1)S(1)} %add_convert_fusion.3), channel_id=1, source_target_pairs={{16,8},{20,12},{24,0},{28,4},{17,9},{21,13},{25,1},{29,5},{18,10},... | collective-permute-start | bytes 1572872 | tf_op jit(solution)/shard_map/ppermute | solution.py:36
  20.2 25.6 %collective-permute-start.17 = (bf16[16,128,128]{2,1,0:T(8,128)(2,1)S(1)}, bf16[16,128,128]{2,1,0:T(8,128)(2,1)S(1)}, u32[]{:S(2)}, u32[]{:S(2)}) collective-permute-start(bf16[16,128,128]{2,1,0:T(8,128)(2,1)S(1)} %get-tuple-element.41), channel_id=1, source_target_pairs={{0,1},{1,0},{2,3},{3,2},{4,5},{5,4},{6,7},{7,6},{8,9},{9,8},{10,11... | collective-permute-start | bytes 1572872 | tf_op jit(solution)/shard_map/ppermute | solution.py:36
  30.2 13.7 %collective-permute-start.5 = (bf16[16,128,128]{2,1,0:T(8,128)(2,1)S(1)}, bf16[16,128,128]{2,1,0:T(8,128)(2,1)S(1)}, u32[]{:S(2)}, u32[]{:S(2)}) collective-permute-start(bf16[16,128,128]{2,1,0:T(8,128)(2,1)S(1)} %add_convert_fusion.6), channel_id=1, source_target_pairs={{0,4},{4,0},{8,12},{12,8},{16,20},{20,16},{24,28},{28,24},{1,5},{5... | collective-permute-start | bytes 1572872 | tf_op jit(solution)/shard_map/ppermute | solution.py:36
  42.5 12.3 %collective-permute-start.16 = (bf16[16,128,128]{2,1,0:T(8,128)(2,1)S(1)}, bf16[16,128,128]{2,1,0:T(8,128)(2,1)S(1)}, u32[]{:S(2)}, u32[]{:S(2)}) collective-permute-start(bf16[16,128,128]{2,1,0:T(8,128)(2,1)S(1)} %fusion), channel_id=1, source_target_pairs={{0,8},{4,12},{8,0},{12,4},{16,24},{20,28},{24,16},{28,20},{1,9},{5... | collective-permute-start | bytes 1572872 | tf_op jit(solution)/shard_map/ppermute | solution.py:36
  42.6 24.9 %collective-permute-start.19 = (bf16[16,128,128]{2,1,0:T(8,128)(2,1)S(1)}, bf16[16,128,128]{2,1,0:T(8,128)(2,1)S(1)}, u32[]{:S(2)}, u32[]{:S(2)}) collective-permute-start(bf16[16,128,128]{2,1,0:T(8,128)(2,1)S(1)} %get-tuple-element.43), channel_id=1, source_target_pairs={{0,1},{1,0},{2,3},{3,2},{4,5},{5,4},{6,7},{7,6},{8,9},{9,8},{10,11... | collective-permute-start | bytes 1572872 | tf_op jit(solution)/shard_map/ppermute | solution.py:36
  44.1 22.0 %collective-permute-start.6 = (bf16[16,128,128]{2,1,0:T(8,128)(2,1)S(1)}, bf16[16,128,128]{2,1,0:T(8,128)(2,1)S(1)}, u32[]{:S(2)}, u32[]{:S(2)}) collective-permute-start(bf16[16,128,128]{2,1,0:T(8,128)(2,1)S(1)} %add_convert_fusion.5), channel_id=1, source_target_pairs={{0,8},{4,12},{8,0},{12,4},{16,24},{20,28},{24,16},{28,20},{1,9},{5... | collective-permute-start | bytes 1572872 | tf_op jit(solution)/shard_map/ppermute | solution.py:36
  55.2 12.4 %collective-permute-start.18 = (bf16[16,128,128]{2,1,0:T(8,128)(2,1)S(1)}, bf16[16,128,128]{2,1,0:T(8,128)(2,1)S(1)}, u32[]{:S(2)}, u32[]{:S(2)}) collective-permute-start(bf16[16,128,128]{2,1,0:T(8,128)(2,1)S(1)} %fusion.2), channel_id=1, source_target_pairs={{0,4},{4,0},{8,12},{12,8},{16,20},{20,16},{24,28},{28,24},{1,5},{5... | collective-permute-start | bytes 1572872 | tf_op jit(solution)/shard_map/ppermute | solution.py:36
  66.2 26.3 %collective-permute-start.11 = (bf16[16,128,128]{2,1,0:T(8,128)(2,1)S(1)}, bf16[16,128,128]{2,1,0:T(8,128)(2,1)S(1)}, u32[]{:S(2)}, u32[]{:S(2)}) collective-permute-start(bf16[16,128,128]{2,1,0:T(8,128)(2,1)S(1)} %add_convert_fusion.4), channel_id=1, source_target_pairs={{0,24},{4,28},{8,16},{12,20},{1,25},{5,29},{9,17},{13,21},{2,26},{... | collective-permute-start | bytes 1572872 | tf_op jit(solution)/shard_map/ppermute | solution.py:36
  68.0 25.8 %collective-permute-start.20 = (bf16[16,128,128]{2,1,0:T(8,128)(2,1)S(1)}, bf16[16,128,128]{2,1,0:T(8,128)(2,1)S(1)}, u32[]{:S(2)}, u32[]{:S(2)}) collective-permute-start(bf16[16,128,128]{2,1,0:T(8,128)(2,1)S(1)} %fusion.4), channel_id=1, source_target_pairs={{0,2},{1,3},{2,0},{3,1},{4,6},{5,7},{6,4},{7,5},{8,10},{9,11},{10,... | collective-permute-start | bytes 1572872 | tf_op jit(solution)/shard_map/ppermute | solution.py:36
  68.6 25.6 %collective-permute-start.7 = (bf16[16,128,128]{2,1,0:T(8,128)(2,1)S(1)}, bf16[16,128,128]{2,1,0:T(8,128)(2,1)S(1)}, u32[]{:S(2)}, u32[]{:S(2)}) collective-permute-start(bf16[16,128,128]{2,1,0:T(8,128)(2,1)S(1)} %get-tuple-element.29), channel_id=1, source_target_pairs={{0,1},{2,3},{4,5},{6,7},{8,9},{10,11},{12,13},{14,15},{16,17},{18,... | collective-permute-start | bytes 1572872 | tf_op jit(solution)/shard_map/ppermute | solution.py:36
  70.0 26.6 %collective-permute-start.8 = (bf16[16,128,128]{2,1,0:T(8,128)(2,1)S(1)}, bf16[16,128,128]{2,1,0:T(8,128)(2,1)S(1)}, u32[]{:S(2)}, u32[]{:S(2)}) collective-permute-start(bf16[16,128,128]{2,1,0:T(8,128)(2,1)S(1)} %collective-permute-done.4.refs_1_), channel_id=1, source_target_pairs={{0,1},{1,0},{2,3},{3,2},{4,5},{5,4},{6,7},{7,6},{8,9},{9,8},{10,11... | collective-permute-start | bytes 1572872 | tf_op jit(solution)/shard_map/ppermute | solution.py:36
  72.3 25.7 %collective-permute-start.9 = (bf16[16,128,128]{2,1,0:T(8,128)(2,1)S(1)}, bf16[16,128,128]{2,1,0:T(8,128)(2,1)S(1)}, u32[]{:S(2)}, u32[]{:S(2)}) collective-permute-start(bf16[16,128,128]{2,1,0:T(8,128)(2,1)S(1)} %collective-permute-done.5.refs_2_), channel_id=1, source_target_pairs={{0,1},{1,0},{2,3},{3,2},{4,5},{5,4},{6,7},{7,6},{8,9},{9,8},{10,11... | collective-permute-start | bytes 1572872 | tf_op jit(solution)/shard_map/ppermute | solution.py:36
  92.5 15.8 %collective-permute-start.10 = (bf16[16,128,128]{2,1,0:T(8,128)(2,1)S(1)}, bf16[16,128,128]{2,1,0:T(8,128)(2,1)S(1)}, u32[]{:S(2)}, u32[]{:S(2)}) collective-permute-start(bf16[16,128,128]{2,1,0:T(8,128)(2,1)S(1)} %collective-permute-done.6.refs_3_), channel_id=1, source_target_pairs={{0,1},{1,0},{2,3},{3,2},{4,5},{5,4},{6,7},{7,6},{8,9},{9,8},{10,11... | collective-permute-start | bytes 1572872 | tf_op jit(solution)/shard_map/ppermute | solution.py:36
  93.8 21.3 %collective-permute-start.12 = (bf16[16,128,128]{2,1,0:T(8,128)(2,1)S(1)}, bf16[16,128,128]{2,1,0:T(8,128)(2,1)S(1)}, u32[]{:S(2)}, u32[]{:S(2)}) collective-permute-start(bf16[16,128,128]{2,1,0:T(8,128)(2,1)S(1)} %collective-permute-done.11.refs_0_), channel_id=1, source_target_pairs={{0,1},{1,0},{2,3},{3,2},{4,5},{5,4},{6,7},{7,6},{8,9},{9,8},{10,11... | collective-permute-start | bytes 1572872 | tf_op jit(solution)/shard_map/ppermute | solution.py:36
  94.2 25.4 %collective-permute-start.21 = (bf16[16,128,128]{2,1,0:T(8,128)(2,1)S(1)}, bf16[16,128,128]{2,1,0:T(8,128)(2,1)S(1)}, u32[]{:S(2)}, u32[]{:S(2)}) collective-permute-start(bf16[16,128,128]{2,1,0:T(8,128)(2,1)S(1)} %get-tuple-element.44), channel_id=1, source_target_pairs={{1,0},{3,2},{5,4},{7,6},{9,8},{11,10},{13,12},{15,14},{17,16},{19,... | collective-permute-start | bytes 1572872 | tf_op jit(solution)/shard_map/ppermute | solution.py:36
  96.6 23.0 %collective-permute-start.23 = (bf16[16,128,128]{2,1,0:T(8,128)(2,1)S(1)}, bf16[16,128,128]{2,1,0:T(8,128)(2,1)S(1)}, u32[]{:S(2)}, u32[]{:S(2)}) collective-permute-start(bf16[16,128,128]{2,1,0:T(8,128)(2,1)S(1)} %get-tuple-element.45), channel_id=1, source_target_pairs={{1,0},{3,2},{5,4},{7,6},{9,8},{11,10},{13,12},{15,14},{17,16},{19,... | collective-permute-start | bytes 1572872 | tf_op jit(solution)/shard_map/ppermute | solution.py:36
  98.0 21.6 %collective-permute-start.22 = (bf16[16,128,128]{2,1,0:T(8,128)(2,1)S(1)}, bf16[16,128,128]{2,1,0:T(8,128)(2,1)S(1)}, u32[]{:S(2)}, u32[]{:S(2)}) collective-permute-start(bf16[16,128,128]{2,1,0:T(8,128)(2,1)S(1)} %fusion.5.refs_0_), channel_id=1, source_target_pairs={{0,1},{1,0},{2,3},{3,2},{4,5},{5,4},{6,7},{7,6},{8,9},{9,8},{10,11... | collective-permute-start | bytes 1572872 | tf_op jit(solution)/shard_map/ppermute | solution.py:36
  (6 other events, 81.8 us)

commit v2 on v1

v2 whole, which is shorter than its diff:
```python
import functools

import jax
import jax.numpy as jnp
from jax import lax
from jax.experimental import pallas as pl
from jax.experimental.pallas import tpu as pltpu
from jax.sharding import PartitionSpec as P


F32 = jnp.float32
BF16 = jnp.bfloat16
CHUNKS = 2
STATE_BATCH = 16
GRAD_BATCH = 8
LOCAL_BATCH = 8
CROSS_BATCH = 8
LAST_BATCH = 8


def level_gain(level):
    if level == 0:
        return 1.0
    return 2.0 ** (-(level - 1) / 2.0)


def dot(left, right, left_dim, right_dim):
    return lax.dot_general(
        left, right, (((left_dim,), (right_dim,)), ((), ())), preferred_element_type=F32
    )


def exchanged(block, axis, mask, sends=None):
    indices = range(lax.axis_size(axis))
    return lax.ppermute(block, axis, [(index, index ^ mask) for index in indices if sends is None or sends(index)])


def plus(left, right):
    return (left.astype(F32) + right.astype(F32)).astype(BF16)


def lanes_of(head, dim):
    return pl.ds(pl.multiple_of(head * dim, dim), dim)


def first_head(info, group, count):
    side = info[0] if group < CHUNKS else 1 - info[0]
    return (side * CHUNKS + group % CHUNKS) * count


def each(count, step, batch):
    batch = min(batch, count)

    def body(at, carry):
        step([at * batch + place for place in range(batch)])
        return carry

    lax.fori_loop(0, count // batch, body, 0)


def state_kernel(info, key, value, own, other, *, dim):
    half = own.shape[0]
    for states, side in ((own, info[0]), (other, 1 - info[0])):

        def step(ids):
            lanes = [lanes_of(side * half + index, dim) for index in ids]
            pairs = [(key[:, at], value[:, at]) for at in lanes]
            outs = [dot(k, v, 0, 0).astype(BF16) for k, v in pairs]
            for index, out in zip(ids, outs):
                states[index] = out

        each(half, step, STATE_BATCH)


def grad_state_kernel(info, query, cot, codes, *outs, dim, first, levels, scales, half, table):
    for at, side in enumerate((info[0], 1 - info[0])):

        def step(ids):
            heads = [side * half + index for index in ids]
            loads = [(query[:, lanes_of(head, dim)], cot[:, lanes_of(head, dim)], codes[head]) for head in heads]
            results = []
            for q, g, code in loads:
                turned, code = q.T.astype(F32), code.astype(F32)
                scaled = [
                    (turned * (code[first + b : first + b + 1] * (scales[b] * info[1 + b].astype(F32)))).astype(BF16)
                    for b in levels
                ]
                results.append(dot(jnp.concatenate(scaled, axis=0), g, 1, 0).astype(BF16))
            for index, grads in zip(ids, results):
                for place in range(len(levels)):
                    which, offset = table[at][place]
                    outs[which][offset + index] = grads[place * dim : (place + 1) * dim]

        each(half, step, STATE_BATCH if len(levels) == 1 else GRAD_BATCH)


def local_kernel(info, query, key, value, cot, codes, out, query_grad, key_grad, value_grad, *, dim, scale, group):
    length = query.shape[0]
    count = out.shape[1] // dim
    source = lax.broadcasted_iota(jnp.int32, (length, length), 0)
    place = lax.broadcasted_iota(jnp.int32, (length, length), 1)
    apart = jnp.bitwise_xor(source, place)
    top = length.bit_length() - 1
    gains = jnp.full((length, length), scale * level_gain(top) / 8.0, F32)
    for level in range(top - 1, -1, -1):
        gains = jnp.where(apart < 2**level, scale * level_gain(level) / 8.0, gains)
    gains = jnp.where(source <= place, gains, 0.0)
    start = first_head(info, group, count)

    def step(ids):
        loads = []
        for index in ids:
            lanes = lanes_of(start + index, dim)
            loads.append((query[:, lanes], key[:, lanes], value[:, lanes], cot[:, lanes], codes[start + index]))
        scores = [(dot(k, q, 1, 1), dot(v, g, 1, 1)) for q, k, v, g, _ in loads]
        results = []
        for (q, k, v, g, code), (score, grad) in zip(loads, scores):
            code = code.astype(F32)
            weight = jnp.broadcast_to(code[top : top + 1], (length, length))
            for level in range(top - 1, -1, -1):
                weight = jnp.where(apart < 2**level, code[level : level + 1], weight)
            weight = weight * gains
            probs, grads = (weight * score).astype(BF16), (weight * grad).astype(BF16)
            results.append((dot(probs, v, 0, 0), dot(grads, k, 0, 0), dot(grads, q, 1, 0), dot(probs, g, 1, 0)))
        for index, result in zip(ids, results):
            here = lanes_of(index, dim)
            out[:, here], query_grad[:, here], key_grad[:, here], value_grad[:, here] = result

    each(count, step, LOCAL_BATCH)


def cross_step(info, query, cot, codes, out_in, query_grad_in, out, query_grad, buckets, *, dim, start, first, levels, scales):
    def step(ids):
        loads = []
        for index in ids:
            lanes, here = lanes_of(start + index, dim), lanes_of(index, dim)
            states = [bucket[offset + index] for bucket, offset in buckets]
            loads.append(
                (query[:, lanes], cot[:, lanes], out_in[:, here], query_grad_in[:, here], codes[start + index], states)
            )
        results = []
        for q, g, added, grad_added, code, states in loads:
            columns = code.astype(F32).T
            row_scales = [columns[:, first + b : first + b + 1] * (scales[b] * info[1 + b].astype(F32)) for b in levels]
            wide_q = jnp.concatenate([(q.astype(F32) * by).astype(BF16) for by in row_scales], axis=1)
            wide_g = jnp.concatenate([(g.astype(F32) * by).astype(BF16) for by in row_scales], axis=1)
            results.append(
                (
                    added + dot(wide_q, jnp.concatenate(states, axis=0), 1, 0),
                    grad_added + dot(wide_g, jnp.concatenate(states, axis=1), 1, 1),
                )
            )
        for index, (left, right) in zip(ids, results):
            here = lanes_of(index, dim)
            out[:, here] = left.astype(out.dtype)
            query_grad[:, here] = right.astype(query_grad.dtype)

    return step


def cross_kernel(info, query, cot, codes, out_in, query_grad_in, *refs, dim, first, levels, scales, group, table):
    out, query_grad = refs[-2:]
    count = out.shape[1] // dim
    step = cross_step(
        info, query, cot, codes, out_in, query_grad_in, out, query_grad,
        [(refs[which], offset) for which, offset in table],
        dim=dim, start=first_head(info, group, count), first=first, levels=levels, scales=scales,
    )
    each(count, step, CROSS_BATCH)


def last_cross_kernel(info, query, cot, codes, out_in, query_grad_in, bucket, *refs, dim, group, first, levels, scales):
    out, query_grad = refs[-2:]
    count = out_in.shape[1] // dim
    start = first_head(info, group, count)
    step = cross_step(
        info, query, cot, codes, out_in, query_grad_in, out, query_grad, [(bucket, 0)],
        dim=dim, start=start, first=first, levels=levels, scales=scales,
    )
    each(count, step, LAST_BATCH)


def pull_kernel(info, key, value, near, key_grad_in, value_grad_in, pull, *refs, dim, group):
    key_grad, value_grad = refs[-2:]
    count = key_grad_in.shape[1] // dim
    offset = (group + CHUNKS) % (2 * CHUNKS) * count
    start = first_head(info, group, count)

    def step(ids):
        loads = []
        for index in ids:
            lanes, here = lanes_of(start + index, dim), lanes_of(index, dim)
            pulled = plus(pull[index], near[offset + index])
            loads.append((key[:, lanes], value[:, lanes], key_grad_in[:, here], value_grad_in[:, here], pulled))
        results = [
            ((keys + dot(v, pulled, 1, 1)).astype(BF16), (values + dot(k, pulled, 1, 0)).astype(BF16))
            for k, v, keys, values, pulled in loads
        ]
        for index, (left, right) in zip(ids, results):
            here = lanes_of(index, dim)
            key_grad[:, here], value_grad[:, here] = left, right

    each(count, step, LAST_BATCH)


def flush_kernel(info, *refs, body, count, dim, groups):
    *refs, left, right, left_piece, right_piece, done = refs
    fixed = len(refs) - 2 * (len(groups) - 1)
    pieces = [*refs[fixed:], left_piece, right_piece]
    copies = []
    for at, group in enumerate(groups):
        columns = pl.ds(pl.multiple_of(first_head(info, group, count) * dim, count * dim), count * dim)
        for which, out in enumerate((left, right)):
            place = 2 * at + which
            copies.append(pltpu.make_async_copy(pieces[place], out.at[:, columns], done.at[place]))
    for copy in copies[:-2]:
        copy.start()
    body(info, *refs[:fixed], left_piece, right_piece)
    for copy in copies[-2:]:
        copy.start()
    for copy in copies:
        copy.wait()


def on_device(query, key, value, cot, level_codes):
    length, width = query.shape
    shard_heads, total_levels, _ = level_codes.shape
    head_count, ctx_count = lax.axis_size("head"), lax.axis_size("ctx")
    heads = shard_heads * head_count
    dim = width // heads
    half = heads // 2
    count = half // CHUNKS
    groups = range(2 * CHUNKS)
    parts = range(CHUNKS)
    tok_bits = length.bit_length() - 1
    head_bits = head_count.bit_length() - 1
    cross = total_levels - tok_bits - 1
    first = tok_bits + 1
    scale = dim**-0.5
    scales = tuple(scale * level_gain(first + b) / 8.0 for b in range(cross))
    ctx_bits = ctx_count.bit_length() - 1
    hops = [("head", 2 << bit) for bit in range(head_bits - 1)] + [("ctx", 1 << bit) for bit in range(ctx_bits - 1)]
    last, step_bit = 1 << (ctx_bits - 1), 1 << (ctx_bits - 2)
    my_head = lax.axis_index("head")
    mine = lax.axis_index("ctx") * head_count + my_head
    bits = [mine // 2**b % 2 for b in range(cross)]
    info = jnp.stack([bits[0], *bits]).astype(jnp.int32)

    padded = -(-total_levels // 16) * 16
    codes = jnp.pad(level_codes.astype(BF16), ((0, 0), (0, padded - total_levels), (0, 0)))
    codes = codes.reshape(shard_heads, padded, head_count, length).transpose(2, 0, 1, 3)
    got = [lax.dynamic_index_in_dim(codes, my_head, keepdims=False)]
    for mask in range(1, head_count):
        got.append(exchanged(lax.dynamic_index_in_dim(codes, my_head ^ mask, keepdims=False), "head", mask))
    slots = []
    for slot in range(head_count):
        chosen = got[0]
        for mask in range(1, head_count):
            chosen = jnp.where(my_head ^ slot == mask, got[mask], chosen)
        slots.append(chosen)
    codes = jnp.concatenate(slots, axis=0)

    in_smem, in_vmem = pl.BlockSpec(memory_space=pltpu.SMEM), pl.BlockSpec(memory_space=pltpu.VMEM)
    wide = pltpu.VMEM((length, count * dim), F32)

    def state_out(number):
        return pltpu.VMEM((number, dim, dim), BF16)

    def run(body, args, outs, work, **more):
        args = [arg if arg is info else pltpu.with_memory_space_constraint(arg, pltpu.VMEM) for arg in args]
        return pl.pallas_call(
            body,
            in_specs=[in_smem if arg is info else in_vmem for arg in args],
            out_shape=outs,
            cost_estimate=pl.CostEstimate(
                flops=int(work * heads * length * dim * dim * 2), bytes_accessed=0, transcendentals=0
            ),
            compiler_params=pltpu.CompilerParams(vmem_limit_bytes=12 << 20),
            **{"out_specs": [in_vmem] * len(outs), **more},
        )(*args)

    def piece(array, offset):
        return lax.slice_in_dim(array, offset, offset + count)

    def grad_states(levels, table, outs):
        return run(
            functools.partial(
                grad_state_kernel, dim=dim, first=first, levels=levels, scales=scales, half=half, table=table
            ),
            [info, query, cot, codes],
            outs,
            len(levels),
        )

    own, other = run(functools.partial(state_kernel, dim=dim), [info, key, value], [state_out(half)] * 2, 1)
    top_own, top_other = grad_states((cross - 1,), (((0, 0),), ((1, 0),)), [state_out(half), state_out(half)])
    rest = cross - 1
    table = (
        ((1, 0),) + tuple((0, half * at) for at in range(rest - 1)),
        ((1, half),) + tuple((1, half * (2 + at)) for at in range(rest - 1)),
    )
    kept, sent = grad_states(tuple(range(rest)), table, [state_out(half * (rest - 1)), state_out(half * (rest + 1))])

    near_own = exchanged(other, "head", 1)
    near_other = exchanged(own, "head", 1)
    top_partner = exchanged(top_other, "head", 1)
    near_grads = exchanged(sent, "head", 1)

    arrived = {}
    running = {}
    tops = {}
    for part in parts:
        running[part] = plus(piece(own, part * count), piece(near_own, part * count))
    for at, (axis, mask) in enumerate(hops):
        for part in parts:
            sends = (lambda i: not i & step_bit) if at + 1 == len(hops) else None
            arrived[at, part] = exchanged(running[part], axis, mask, sends)
            running[part] = plus(running[part], arrived[at, part])
    for part in parts:
        over = exchanged(running[part], "ctx", last | step_bit, lambda i: not i & last and bool(i & step_bit))
        relay = exchanged(over, "ctx", step_bit, lambda i: i & last and not i & step_bit)
        tops[part] = plus(over, relay)
        tops[part + CHUNKS] = exchanged(tops[part], "head", 1)

    pulled = {}
    for part in parts:
        grad = plus(piece(top_own, part * count), piece(top_partner, part * count))
        relay = exchanged(grad, "ctx", step_bit, lambda i: i & last and i & step_bit)
        grad = plus(grad, relay)
        pulled[part] = exchanged(grad, "ctx", last | step_bit, lambda i: i & last and not i & step_bit)
    offsets = [at * half + part * count for at in range(len(hops)) for part in parts]
    pair_grads = lax.optimization_barrier(
        [plus(piece(kept, offset), piece(near_grads, 2 * half + offset)) for offset in offsets]
    )
    for at in range(len(hops) - 1, -1, -1):
        axis, mask = hops[at]
        for part in parts:
            grad = pair_grads[at * CHUNKS + part]
            grad = plus(pulled[part], grad)
            grad = exchanged(grad, axis, mask, (lambda i: i & step_bit) if at + 1 == len(hops) else None)
            pulled[part] = plus(pulled[part], grad)
    for part in parts:
        pulled[part + CHUNKS] = exchanged(pulled[part], "head", 1)

    sums = {}
    for group in groups:
        sums[group] = list(
            run(
                functools.partial(local_kernel, dim=dim, scale=scale, group=group),
                [info, query, key, value, cot, codes],
                [wide] * 4,
                6 / len(groups),
            )
        )

    for part in parts:
        shared = jnp.concatenate([arrived[at, part] for at in range(len(hops))])
        shared = exchanged(shared, "head", 1)
        for group in (part, part + CHUNKS):
            offset = part * count
            if group == part:
                refs = [near_own] + [arrived[at, part] for at in range(len(hops))]
                table = ((0, offset),) + tuple((1 + at, 0) for at in range(len(hops)))
            else:
                refs = [near_other, shared]
                table = ((0, offset),) + tuple((1, at * count) for at in range(len(hops)))
            sums[group][:2] = run(
                functools.partial(
                    cross_kernel, dim=dim, first=first, levels=tuple(range(rest)), scales=scales, group=group,
                    table=table,
                ),
                [info, query, cot, codes, *sums[group][:2], *refs],
                [wide] * 2,
                2 * rest / len(groups),
            )

    def finished(body, args, **more):
        order = [at for part in parts for at in (part, part + CHUNKS)]
        small = pltpu.VMEM((length, count * dim), BF16)
        pieces = []
        for group in order[:-1]:
            kernel = functools.partial(body, dim=dim, group=group, **more)
            pieces += run(kernel, [info, *args(group)], [small] * 2, 2 / len(groups))
        kernel = functools.partial(body, dim=dim, group=order[-1], **more)
        return run(
            functools.partial(flush_kernel, body=kernel, count=count, dim=dim, groups=order),
            [info, *args(order[-1]), *pieces],
            [jax.ShapeDtypeStruct((length, width), BF16)] * 2,
            2 / len(groups),
            out_specs=[pl.BlockSpec(memory_space=pl.ANY)] * 2,
            scratch_shapes=[small, small, pltpu.SemaphoreType.DMA((2 * len(order),))],
        )

    attended, query_grad = finished(
        last_cross_kernel,
        lambda group: [query, cot, codes, *sums[group][:2], tops[group]],
        first=first,
        levels=(cross - 1,),
        scales=scales,
    )
    key_grad, value_grad = finished(
        pull_kernel, lambda group: [key, value, near_grads, *sums[group][2:], pulled[group]]
    )
    return attended, query_grad, key_grad, value_grad


def solution(mesh):
    rows = P(("ctx", "head"), None)
    return jax.shard_map(
        on_device,
        mesh=mesh,
        in_specs=(rows, rows, rows, rows, P("head", None, "ctx")),
        out_specs=(rows, rows, rows, rows),
        check_vma=False,
    )
```

time: 124 us -> 125 us (level)
  the two profiles are of different devices: /device:TPU:17 before, /device:TPU:0 now
where the time goes in v2:
time: 125 us
  waiting for transfers between devices  59.7 us (48%)
  Pallas kernels  29.9 us (24%)
  starting transfers between devices  27 us (22%)
  other arithmetic  3.86 us (3%)
  local copies, waits for them, and re-layouts  2.63 us (2%)
  between operations  1.43 us (1%)
    ppermute x33, waiting for transfers between devices, exchanged(): lax.ppermute(block, axis, [(index, index ^ mask) for index in indices if...  59.7 us
    pallas_call x19, Pallas kernels, run(): pl.pallas_call(body, in_specs=[in_smem if arg is info else in_vmem for ar...  29.9 us
    ppermute x33, starting transfers between devices, exchanged(): lax.ppermute(block, axis, [(index, index ^ mask) for index in indices if...  27 us
    convert_element_type x21, other arithmetic, plus(): return (left.astype(F32) + right.astype(F32)).astype(BF16)  2.54 us
  transfers between devices with their start and end apart: 33, of which 12 were waited for; matrix products, arithmetic and copies ran while one was open for 2% of the time, Pallas kernels for 22%

profile of v2, /device:TPU:0, one launch (start us, length us, event | category | flops | bytes accessed | tf_op | source)
XLA Modules:
  0.0 124.5 jit_solution(13648240888528132039)
XLA Ops:
  1.9 2.5 %collective-permute-start = (bf16[8,16,128]{2,1,0:T(8,128)(2,1)S(1)}, bf16[8,16,128]{2,1,0:T(8,128)(2,1)S(1)}, u32[]{:S(2)}, u32[]{:S(2)}) collective-permute-start(bf16[8,16,128]{2,1,0:T(8,128)(2,1)S(1)} %bitcast.26), channel_id=1, source_target_pairs={{0,3},{1,2},{2,1},{3,0},{4,7},{5,6},{6,5},{7,4},{8,11},{9,10},{10,... | collective-permute-start | bytes 98312 | tf_op jit(solution)/shard_map/ppermute | solution.py:35
  7.6 2.1 %shard_map.85 = (bf16[16,128,128]{2,1,0:T(8,128)(2,1)S(1)}, bf16[16,128,128]{2,1,0:T(8,128)(2,1)}) custom-call(s32[6]{0:T(128)S(1)} %stack.24.info, bf16[128,4096]{1,0:T(8,128)(2,1)S(1)} %copy-done.2, bf16[128,4096]{1,0:T(8,128)(2,1)S(1)} %copy-done.4), custom_call_target="tpu_custom_call" | custom-call | flops 134217728 | tf_op jit(solution)/shard_map/pallas_call | solution.py:271
  11.7 2.5 %shard_map.97 = (bf16[48,128,128]{2,1,0:T(8,128)(2,1)S(1)}, bf16[80,128,128]{2,1,0:T(8,128)(2,1)S(1)}) custom-call(s32[6]{0:T(128)S(1)} %stack.24.info, bf16[128,4096]{1,0:T(8,128)(2,1)S(1)} %copy-done, bf16[128,4096]{1,0:T(8,128)(2,1)S(1)} %copy-done.1, bf16[32,16,128]{2,1,0:T(8,128)(2,1)S(1)} %pad_maximum_fusion.2.codes.refs_2_), custom_call_target="tpu_custom_call" | custom-call | flops 536870912 | tf_op jit(solution)/shard_map/pallas_call | solution.py:271
  17.8 6.3 %collective-permute-done.5.refs_1_ = bf16[8,128,128]{2,1,0:T(8,128)(2,1)S(1)} collective-permute-done((bf16[8,128,128]{2,1,0:T(8,128)(2,1)S(1)}, bf16[8,128,128]{2,1,0:T(8,128)(2,1)S(1)}, u32[]{:S(2)}, u32[]{:S(2)}) %collective-permute-start.5) | collective-permute-done | bytes 262176 | tf_op jit(solution)/shard_map/ppermute | solution.py:35
  24.9 4.0 %collective-permute-done.12.refs_1_ = bf16[8,128,128]{2,1,0:T(8,128)(2,1)S(1)} collective-permute-done((bf16[8,128,128]{2,1,0:T(8,128)(2,1)S(1)}, bf16[8,128,128]{2,1,0:T(8,128)(2,1)S(1)}, u32[]{:S(2)}, u32[]{:S(2)}) %collective-permute-start.12) | collective-permute-done | bytes 262176 | tf_op jit(solution)/shard_map/ppermute | solution.py:35
  28.9 1.7 %collective-permute-start.6 = (bf16[8,128,128]{2,1,0:T(8,128)(2,1)S(1)}, bf16[8,128,128]{2,1,0:T(8,128)(2,1)S(1)}, u32[]{:S(2)}, u32[]{:S(2)}) collective-permute-start(bf16[8,128,128]{2,1,0:T(8,128)(2,1)S(1)} %add_convert_fusion.18), channel_id=1, source_target_pairs={{0,4},{4,0},{8,12},{12,8},{16,20},{20,16},{24,28},{28,24},{1,5},{5... | collective-permute-start | bytes 786440 | tf_op jit(solution)/shard_map/ppermute | solution.py:35
  31.1 6.9 %collective-permute-done.6.refs_2_ = bf16[8,128,128]{2,1,0:T(8,128)(2,1)S(1)} collective-permute-done((bf16[8,128,128]{2,1,0:T(8,128)(2,1)S(1)}, bf16[8,128,128]{2,1,0:T(8,128)(2,1)S(1)}, u32[]{:S(2)}, u32[]{:S(2)}) %collective-permute-start.6) | collective-permute-done | bytes 262176 | tf_op jit(solution)/shard_map/ppermute | solution.py:35
  38.8 3.3 %collective-permute-done.13.refs_2_ = bf16[8,128,128]{2,1,0:T(8,128)(2,1)S(1)} collective-permute-done((bf16[8,128,128]{2,1,0:T(8,128)(2,1)S(1)}, bf16[8,128,128]{2,1,0:T(8,128)(2,1)S(1)}, u32[]{:S(2)}, u32[]{:S(2)}) %collective-permute-start.13) | collective-permute-done | bytes 262176 | tf_op jit(solution)/shard_map/ppermute | solution.py:35
  42.1 3.7 %collective-permute-start.7 = (bf16[8,128,128]{2,1,0:T(8,128)(2,1)S(1)}, bf16[8,128,128]{2,1,0:T(8,128)(2,1)S(1)}, u32[]{:S(2)}, u32[]{:S(2)}) collective-permute-start(bf16[8,128,128]{2,1,0:T(8,128)(2,1)S(1)} %add_convert_fusion.17), channel_id=1, source_target_pairs={{0,8},{4,12},{16,24},{20,28},{1,9},{5,13},{17,25},{21,29},{2,10},{... | collective-permute-start | bytes 786440 | tf_op jit(solution)/shard_map/ppermute | solution.py:35
  47.3 5.2 %collective-permute-done.7.refs_3_ = bf16[8,128,128]{2,1,0:T(8,128)(2,1)S(1)} collective-permute-done((bf16[8,128,128]{2,1,0:T(8,128)(2,1)S(1)}, bf16[8,128,128]{2,1,0:T(8,128)(2,1)S(1)}, u32[]{:S(2)}, u32[]{:S(2)}) %collective-permute-start.7) | collective-permute-done | bytes 262176 | tf_op jit(solution)/shard_map/ppermute | solution.py:35
  53.2 2.5 %collective-permute-done.14.refs_3_ = bf16[8,128,128]{2,1,0:T(8,128)(2,1)S(1)} collective-permute-done((bf16[8,128,128]{2,1,0:T(8,128)(2,1)S(1)}, bf16[8,128,128]{2,1,0:T(8,128)(2,1)S(1)}, u32[]{:S(2)}, u32[]{:S(2)}) %collective-permute-start.14) | collective-permute-done | bytes 262176 | tf_op jit(solution)/shard_map/ppermute | solution.py:35
  60.8 10.9 %collective-permute-done.29 = bf16[8,128,128]{2,1,0:T(8,128)(2,1)S(1)} collective-permute-done((bf16[8,128,128]{2,1,0:T(8,128)(2,1)S(1)}, bf16[8,128,128]{2,1,0:T(8,128)(2,1)S(1)}, u32[]{:S(2)}, u32[]{:S(2)}) %collective-permute-start.29) | collective-permute-done | bytes 262176 | tf_op jit(solution)/shard_map/ppermute | solution.py:35
  72.5 3.2 %collective-permute-done.23 = bf16[8,128,128]{2,1,0:T(8,128)(2,1)S(1)} collective-permute-done((bf16[8,128,128]{2,1,0:T(8,128)(2,1)S(1)}, bf16[8,128,128]{2,1,0:T(8,128)(2,1)S(1)}, u32[]{:S(2)}, u32[]{:S(2)}) %collective-permute-start.23) | collective-permute-done | bytes 262176 | tf_op jit(solution)/shard_map/ppermute | solution.py:35
  78.1 6.8 %collective-permute-done.30 = bf16[8,128,128]{2,1,0:T(8,128)(2,1)S(1)} collective-permute-done((bf16[8,128,128]{2,1,0:T(8,128)(2,1)S(1)}, bf16[8,128,128]{2,1,0:T(8,128)(2,1)S(1)}, u32[]{:S(2)}, u32[]{:S(2)}) %collective-permute-start.30) | collective-permute-done | bytes 262176 | tf_op jit(solution)/shard_map/ppermute | solution.py:35
  85.9 2.1 %collective-permute-done.24 = bf16[8,128,128]{2,1,0:T(8,128)(2,1)S(1)} collective-permute-done((bf16[8,128,128]{2,1,0:T(8,128)(2,1)S(1)}, bf16[8,128,128]{2,1,0:T(8,128)(2,1)S(1)}, u32[]{:S(2)}, u32[]{:S(2)}) %collective-permute-start.24) | collective-permute-done | bytes 262176 | tf_op jit(solution)/shard_map/ppermute | solution.py:35
  88.0 1.6 %collective-permute-start.31 = (bf16[8,128,128]{2,1,0:T(8,128)(2,1)S(1)}, bf16[8,128,128]{2,1,0:T(8,128)(2,1)S(1)}, u32[]{:S(2)}, u32[]{:S(2)}) collective-permute-start(bf16[8,128,128]{2,1,0:T(8,128)(2,1)S(1)} %fusion.10), channel_id=1, source_target_pairs={{0,2},{1,3},{2,0},{3,1},{4,6},{5,7},{6,4},{7,5},{8,10},{9,11},{10,... | collective-permute-start | bytes 786440 | tf_op jit(solution)/shard_map/ppermute | solution.py:35
  90.4 6.3 %collective-permute-done.31 = bf16[8,128,128]{2,1,0:T(8,128)(2,1)S(1)} collective-permute-done((bf16[8,128,128]{2,1,0:T(8,128)(2,1)S(1)}, bf16[8,128,128]{2,1,0:T(8,128)(2,1)S(1)}, u32[]{:S(2)}, u32[]{:S(2)}) %collective-permute-start.31) | collective-permute-done | bytes 262176 | tf_op jit(solution)/shard_map/ppermute | solution.py:35
  97.4 2.1 %collective-permute-done.25 = bf16[8,128,128]{2,1,0:T(8,128)(2,1)S(1)} collective-permute-done((bf16[8,128,128]{2,1,0:T(8,128)(2,1)S(1)}, bf16[8,128,128]{2,1,0:T(8,128)(2,1)S(1)}, u32[]{:S(2)}, u32[]{:S(2)}) %collective-permute-start.25) | collective-permute-done | bytes 262176 | tf_op jit(solution)/shard_map/ppermute | solution.py:35
  106.0 1.7 %shard_map.94 = (f32[128,1024]{1,0:T(8,128)S(1)}, f32[128,1024]{1,0:T(8,128)S(1)}) custom-call(s32[6]{0:T(128)S(1)} %stack.24.info, bf16[128,4096]{1,0:T(8,128)(2,1)S(1)} %copy-done, bf16[128,4096]{1,0:T(8,128)(2,1)S(1)} %copy-done.1, bf16[32,16,128]{2,1,0:T(8,128)(2,1)S(1)} %pad_maximum_fusion.2.codes.refs_2_, f32[128,1024]{1,0:T(8,128)S(1)} %get-tuple-element.74.out_in, ...), custom_call_target="tpu_custom_call" | custom-call | flops 268435456 | tf_op jit(solution)/shard_map/pallas_call | solution.py:271
  107.7 1.7 %shard_map.88 = (f32[128,1024]{1,0:T(8,128)S(1)}, f32[128,1024]{1,0:T(8,128)S(1)}) custom-call(s32[6]{0:T(128)S(1)} %stack.24.info, bf16[128,4096]{1,0:T(8,128)(2,1)S(1)} %copy-done, bf16[128,4096]{1,0:T(8,128)(2,1)S(1)} %copy-done.1, bf16[32,16,128]{2,1,0:T(8,128)(2,1)S(1)} %pad_maximum_fusion.2.codes.refs_2_, f32[128,1024]{1,0:T(8,128)S(1)} %get-tuple-element.62.out_in, ...), custom_call_target="tpu_custom_call" | custom-call | flops 268435456 | tf_op jit(solution)/shard_map/pallas_call | solution.py:271
  112.1 1.7 %shard_map.91 = (f32[128,1024]{1,0:T(8,128)S(1)}, f32[128,1024]{1,0:T(8,128)S(1)}) custom-call(s32[6]{0:T(128)S(1)} %stack.24.info, bf16[128,4096]{1,0:T(8,128)(2,1)S(1)} %copy-done, bf16[128,4096]{1,0:T(8,128)(2,1)S(1)} %copy-done.1, bf16[32,16,128]{2,1,0:T(8,128)(2,1)S(1)} %pad_maximum_fusion.2.codes.refs_2_, f32[128,1024]{1,0:T(8,128)S(1)} %get-tuple-element.68.out_in, ...), custom_call_target="tpu_custom_call" | custom-call | flops 268435456 | tf_op jit(solution)/shard_map/pallas_call | solution.py:271
  115.1 1.7 %shard_map.86 = (f32[128,1024]{1,0:T(8,128)S(1)}, f32[128,1024]{1,0:T(8,128)S(1)}) custom-call(s32[6]{0:T(128)S(1)} %stack.24.info, bf16[128,4096]{1,0:T(8,128)(2,1)S(1)} %copy-done, bf16[128,4096]{1,0:T(8,128)(2,1)S(1)} %copy-done.1, bf16[32,16,128]{2,1,0:T(8,128)(2,1)S(1)} %pad_maximum_fusion.2.codes.refs_2_, f32[128,1024]{1,0:T(8,128)S(1)} %get-tuple-element.56.out_in, ...), custom_call_target="tpu_custom_call" | custom-call | flops 268435456 | tf_op jit(solution)/shard_map/pallas_call | solution.py:271
  116.8 2.6 %shard_map.96 = (bf16[128,4096]{1,0:T(8,128)(2,1)}, bf16[128,4096]{1,0:T(8,128)(2,1)}) custom-call(s32[6]{0:T(128)S(1)} %stack.24.info, bf16[128,4096]{1,0:T(8,128)(2,1)S(1)} %copy-done, bf16[128,4096]{1,0:T(8,128)(2,1)S(1)} %copy-done.1, bf16[32,16,128]{2,1,0:T(8,128)(2,1)S(1)} %pad_maximum_fusion.2.codes.refs_2_, ...), custom_call_target="tpu_custom_call" | custom-call | flops 67108864 | tf_op jit(solution)/shard_map/pallas_call | solution.py:271
  122.2 2.2 %shard_map.102 = (bf16[128,4096]{1,0:T(8,128)(2,1)}, bf16[128,4096]{1,0:T(8,128)(2,1)}) custom-call(s32[6]{0:T(128)S(1)} %stack.24.info, bf16[128,4096]{1,0:T(8,128)(2,1)S(1)} %copy-done.3, bf16[128,4096]{1,0:T(8,128)(2,1)S(1)} %copy-done.5, bf16[80,128,128]{2,1,0:T(8,128)(2,1)S(1)} %collective-permute-done.19.near.refs_2_, ...), custom_call_target="tpu_custom_call" | custom-call | flops 67108864 | tf_op jit(solution)/shard_map/pallas_call | solution.py:271
  (105 shorter events, 38.0 us)
Async XLA Ops:
  14.3 42.3 %collective-permute-start.19 = (bf16[80,128,128]{2,1,0:T(8,128)(2,1)S(1)}, bf16[80,128,128]{2,1,0:T(8,128)(2,1)S(1)}, u32[]{:S(2)}, u32[]{:S(2)}) collective-permute-start(bf16[80,128,128]{2,1,0:T(8,128)(2,1)S(1)} %get-tuple-element.82), channel_id=1, source_target_pairs={{0,1},{1,0},{2,3},{3,2},{4,5},{5,4},{6,7},{7,6},{8,9},{9,8},{10,11... | collective-permute-start | bytes 7864328 | tf_op jit(solution)/shard_map/ppermute | solution.py:35
  14.9 9.2 %collective-permute-start.5 = (bf16[8,128,128]{2,1,0:T(8,128)(2,1)S(1)}, bf16[8,128,128]{2,1,0:T(8,128)(2,1)S(1)}, u32[]{:S(2)}, u32[]{:S(2)}) collective-permute-start(bf16[8,128,128]{2,1,0:T(8,128)(2,1)S(1)} %get-tuple-element.117), channel_id=1, source_target_pairs={{0,2},{1,3},{2,0},{3,1},{4,6},{5,7},{6,4},{7,5},{8,10},{9,11},{10,... | collective-permute-start | bytes 786440 | tf_op jit(solution)/shard_map/ppermute | solution.py:35
  16.3 80.5 %collective-permute-start.3 = (bf16[16,128,128]{2,1,0:T(8,128)(2,1)S(1)}, bf16[16,128,128]{2,1,0:T(8,128)(2,1)S(1)}, u32[]{:S(2)}, u32[]{:S(2)}) collective-permute-start(bf16[16,128,128]{2,1,0:T(8,128)(2,1)S(1)} %get-tuple-element.58), channel_id=1, source_target_pairs={{0,1},{1,0},{2,3},{3,2},{4,5},{5,4},{6,7},{7,6},{8,9},{9,8},{10,11... | collective-permute-start | bytes 1572872 | tf_op jit(solution)/shard_map/ppermute | solution.py:35
  16.4 12.5 %collective-permute-start.12 = (bf16[8,128,128]{2,1,0:T(8,128)(2,1)S(1)}, bf16[8,128,128]{2,1,0:T(8,128)(2,1)S(1)}, u32[]{:S(2)}, u32[]{:S(2)}) collective-permute-start(bf16[8,128,128]{2,1,0:T(8,128)(2,1)S(1)} %get-tuple-element.116), channel_id=1, source_target_pairs={{0,2},{1,3},{2,0},{3,1},{4,6},{5,7},{6,4},{7,5},{8,10},{9,11},{10,... | collective-permute-start | bytes 786440 | tf_op jit(solution)/shard_map/ppermute | solution.py:35
  17.1 13.5 %collective-permute-start.21 = (bf16[8,128,128]{2,1,0:T(8,128)(2,1)S(1)}, bf16[8,128,128]{2,1,0:T(8,128)(2,1)S(1)}, u32[]{:S(2)}, u32[]{:S(2)}) collective-permute-start(bf16[8,128,128]{2,1,0:T(8,128)(2,1)S(1)} %get-tuple-element.115), channel_id=1, source_target_pairs={{24,16},{28,20},{25,17},{29,21},{26,18},{30,22},{27,19},{31,23}} | collective-permute-start | bytes 786440 | tf_op jit(solution)/shard_map/ppermute | solution.py:35
  24.1 21.8 %collective-permute-start.27 = (bf16[8,128,128]{2,1,0:T(8,128)(2,1)S(1)}, bf16[8,128,128]{2,1,0:T(8,128)(2,1)S(1)}, u32[]{:S(2)}, u32[]{:S(2)}) collective-permute-start(bf16[8,128,128]{2,1,0:T(8,128)(2,1)S(1)} %get-tuple-element.114), channel_id=1, source_target_pairs={{24,16},{28,20},{25,17},{29,21},{26,18},{30,22},{27,19},{31,23}} | collective-permute-start | bytes 786440 | tf_op jit(solution)/shard_map/ppermute | solution.py:35
  28.9 9.2 %collective-permute-start.6 = (bf16[8,128,128]{2,1,0:T(8,128)(2,1)S(1)}, bf16[8,128,128]{2,1,0:T(8,128)(2,1)S(1)}, u32[]{:S(2)}, u32[]{:S(2)}) collective-permute-start(bf16[8,128,128]{2,1,0:T(8,128)(2,1)S(1)} %add_convert_fusion.18), channel_id=1, source_target_pairs={{0,4},{4,0},{8,12},{12,8},{16,20},{20,16},{24,28},{28,24},{1,5},{5... | collective-permute-start | bytes 786440 | tf_op jit(solution)/shard_map/ppermute | solution.py:35
  30.6 11.4 %collective-permute-start.13 = (bf16[8,128,128]{2,1,0:T(8,128)(2,1)S(1)}, bf16[8,128,128]{2,1,0:T(8,128)(2,1)S(1)}, u32[]{:S(2)}, u32[]{:S(2)}) collective-permute-start(bf16[8,128,128]{2,1,0:T(8,128)(2,1)S(1)} %add_convert_fusion.13), channel_id=1, source_target_pairs={{0,4},{4,0},{8,12},{12,8},{16,20},{20,16},{24,28},{28,24},{1,5},{5... | collective-permute-start | bytes 786440 | tf_op jit(solution)/shard_map/ppermute | solution.py:35
  38.1 20.5 %collective-permute-start.22 = (bf16[8,128,128]{2,1,0:T(8,128)(2,1)S(1)}, bf16[8,128,128]{2,1,0:T(8,128)(2,1)S(1)}, u32[]{:S(2)}, u32[]{:S(2)}) collective-permute-start(bf16[8,128,128]{2,1,0:T(8,128)(2,1)S(1)} %add_convert_fusion.8), channel_id=1, source_target_pairs={{16,8},{20,12},{17,9},{21,13},{18,10},{22,14},{19,11},{23,15}} | collective-permute-start | bytes 786440 | tf_op jit(solution)/shard_map/ppermute | solution.py:35
  42.1 10.4 %collective-permute-start.7 = (bf16[8,128,128]{2,1,0:T(8,128)(2,1)S(1)}, bf16[8,128,128]{2,1,0:T(8,128)(2,1)S(1)}, u32[]{:S(2)}, u32[]{:S(2)}) collective-permute-start(bf16[8,128,128]{2,1,0:T(8,128)(2,1)S(1)} %add_convert_fusion.17), channel_id=1, source_target_pairs={{0,8},{4,12},{16,24},{20,28},{1,9},{5,13},{17,25},{21,29},{2,10},{... | collective-permute-start | bytes 786440 | tf_op jit(solution)/shard_map/ppermute | solution.py:35
  45.9 9.8 %collective-permute-start.14 = (bf16[8,128,128]{2,1,0:T(8,128)(2,1)S(1)}, bf16[8,128,128]{2,1,0:T(8,128)(2,1)S(1)}, u32[]{:S(2)}, u32[]{:S(2)}) collective-permute-start(bf16[8,128,128]{2,1,0:T(8,128)(2,1)S(1)} %add_convert_fusion.12), channel_id=1, source_target_pairs={{0,8},{4,12},{16,24},{20,28},{1,9},{5,13},{17,25},{21,29},{2,10},{... | collective-permute-start | bytes 786440 | tf_op jit(solution)/shard_map/ppermute | solution.py:35
  56.5 43.1 %collective-permute-start.17 = (bf16[24,128,128]{2,1,0:T(8,128)(2,1)S(1)}, bf16[24,128,128]{2,1,0:T(8,128)(2,1)S(1)}, u32[]{:S(2)}, u32[]{:S(2)}) collective-permute-start(bf16[24,128,128]{2,1,0:T(8,128)(2,1)S(1)} %pad_maximum_fusion.1), channel_id=1, source_target_pairs={{0,1},{1,0},{2,3},{3,2},{4,5},{5,4},{6,7},{7,6},{8,9},{9,8},{10,11... | collective-permute-start | bytes 2359304 | tf_op jit(solution)/shard_map/ppermute | solution.py:35
  57.3 14.4 %collective-permute-start.29 = (bf16[8,128,128]{2,1,0:T(8,128)(2,1)S(1)}, bf16[8,128,128]{2,1,0:T(8,128)(2,1)S(1)}, u32[]{:S(2)}, u32[]{:S(2)}) collective-permute-start(bf16[8,128,128]{2,1,0:T(8,128)(2,1)S(1)} %fusion.6), channel_id=1, source_target_pairs={{8,0},{12,4},{24,16},{28,20},{9,1},{13,5},{25,17},{29,21},{10,2},{... | collective-permute-start | bytes 786440 | tf_op jit(solution)/shard_map/ppermute | solution.py:35
  58.7 17.0 %collective-permute-start.23 = (bf16[8,128,128]{2,1,0:T(8,128)(2,1)S(1)}, bf16[8,128,128]{2,1,0:T(8,128)(2,1)S(1)}, u32[]{:S(2)}, u32[]{:S(2)}) collective-permute-start(bf16[8,128,128]{2,1,0:T(8,128)(2,1)S(1)} %fusion), channel_id=1, source_target_pairs={{8,0},{12,4},{24,16},{28,20},{9,1},{13,5},{25,17},{29,21},{10,2},{... | collective-permute-start | bytes 786440 | tf_op jit(solution)/shard_map/ppermute | solution.py:35
  60.1 17.9 %collective-permute-start.15 = (bf16[8,128,128]{2,1,0:T(8,128)(2,1)S(1)}, bf16[8,128,128]{2,1,0:T(8,128)(2,1)S(1)}, u32[]{:S(2)}, u32[]{:S(2)}) collective-permute-start(bf16[8,128,128]{2,1,0:T(8,128)(2,1)S(1)} %add_convert_fusion.11), channel_id=1, source_target_pairs={{8,16},{12,20},{9,17},{13,21},{10,18},{14,22},{11,19},{15,23}} | collective-permute-start | bytes 786440 | tf_op jit(solution)/shard_map/ppermute | solution.py:35
  75.7 9.2 %collective-permute-start.30 = (bf16[8,128,128]{2,1,0:T(8,128)(2,1)S(1)}, bf16[8,128,128]{2,1,0:T(8,128)(2,1)S(1)}, u32[]{:S(2)}, u32[]{:S(2)}) collective-permute-start(bf16[8,128,128]{2,1,0:T(8,128)(2,1)S(1)} %fusion.8), channel_id=1, source_target_pairs={{0,4},{4,0},{8,12},{12,8},{16,20},{20,16},{24,28},{28,24},{1,5},{5... | collective-permute-start | bytes 786440 | tf_op jit(solution)/shard_map/ppermute | solution.py:35
  77.4 10.7 %collective-permute-start.24 = (bf16[8,128,128]{2,1,0:T(8,128)(2,1)S(1)}, bf16[8,128,128]{2,1,0:T(8,128)(2,1)S(1)}, u32[]{:S(2)}, u32[]{:S(2)}) collective-permute-start(bf16[8,128,128]{2,1,0:T(8,128)(2,1)S(1)} %fusion.2), channel_id=1, source_target_pairs={{0,4},{4,0},{8,12},{12,8},{16,20},{20,16},{24,28},{28,24},{1,5},{5... | collective-permute-start | bytes 786440 | tf_op jit(solution)/shard_map/ppermute | solution.py:35
  78.0 37.1 %collective-permute-start.8 = (bf16[24,128,128]{2,1,0:T(8,128)(2,1)S(1)}, bf16[24,128,128]{2,1,0:T(8,128)(2,1)S(1)}, u32[]{:S(2)}, u32[]{:S(2)}) collective-permute-start(bf16[24,128,128]{2,1,0:T(8,128)(2,1)S(1)} %pad_maximum_fusion), channel_id=1, source_target_pairs={{0,1},{1,0},{2,3},{3,2},{4,5},{5,4},{6,7},{7,6},{8,9},{9,8},{10,11... | collective-permute-start | bytes 2359304 | tf_op jit(solution)/shard_map/ppermute | solution.py:35
  88.0 8.7 %collective-permute-start.31 = (bf16[8,128,128]{2,1,0:T(8,128)(2,1)S(1)}, bf16[8,128,128]{2,1,0:T(8,128)(2,1)S(1)}, u32[]{:S(2)}, u32[]{:S(2)}) collective-permute-start(bf16[8,128,128]{2,1,0:T(8,128)(2,1)S(1)} %fusion.10), channel_id=1, source_target_pairs={{0,2},{1,3},{2,0},{3,1},{4,6},{5,7},{6,4},{7,5},{8,10},{9,11},{10,... | collective-permute-start | bytes 786440 | tf_op jit(solution)/shard_map/ppermute | solution.py:35
  89.8 9.7 %collective-permute-start.25 = (bf16[8,128,128]{2,1,0:T(8,128)(2,1)S(1)}, bf16[8,128,128]{2,1,0:T(8,128)(2,1)S(1)}, u32[]{:S(2)}, u32[]{:S(2)}) collective-permute-start(bf16[8,128,128]{2,1,0:T(8,128)(2,1)S(1)} %fusion.4), channel_id=1, source_target_pairs={{0,2},{1,3},{2,0},{3,1},{4,6},{5,7},{6,4},{7,5},{8,10},{9,11},{10,... | collective-permute-start | bytes 786440 | tf_op jit(solution)/shard_map/ppermute | solution.py:35
  96.7 17.0 %collective-permute-start.18 = (bf16[8,128,128]{2,1,0:T(8,128)(2,1)S(1)}, bf16[8,128,128]{2,1,0:T(8,128)(2,1)S(1)}, u32[]{:S(2)}, u32[]{:S(2)}) collective-permute-start(bf16[8,128,128]{2,1,0:T(8,128)(2,1)S(1)} %add_convert_fusion.10.bucket), channel_id=1, source_target_pairs={{0,1},{1,0},{2,3},{3,2},{4,5},{5,4},{6,7},{7,6},{8,9},{9,8},{10,11... | collective-permute-start | bytes 786440 | tf_op jit(solution)/shard_map/ppermute | solution.py:35
  96.9 19.9 %collective-permute-start.11 = (bf16[8,128,128]{2,1,0:T(8,128)(2,1)S(1)}, bf16[8,128,128]{2,1,0:T(8,128)(2,1)S(1)}, u32[]{:S(2)}, u32[]{:S(2)}) collective-permute-start(bf16[8,128,128]{2,1,0:T(8,128)(2,1)S(1)} %add_convert_fusion.15.bucket), channel_id=1, source_target_pairs={{0,1},{1,0},{2,3},{3,2},{4,5},{5,4},{6,7},{7,6},{8,9},{9,8},{10,11... | collective-permute-start | bytes 786440 | tf_op jit(solution)/shard_map/ppermute | solution.py:35
  99.5 21.7 %collective-permute-start.32 = (bf16[8,128,128]{2,1,0:T(8,128)(2,1)S(1)}, bf16[8,128,128]{2,1,0:T(8,128)(2,1)S(1)}, u32[]{:S(2)}, u32[]{:S(2)}) collective-permute-start(bf16[8,128,128]{2,1,0:T(8,128)(2,1)S(1)} %fusion.11.pull), channel_id=1, source_target_pairs={{0,1},{1,0},{2,3},{3,2},{4,5},{5,4},{6,7},{7,6},{8,9},{9,8},{10,11... | collective-permute-start | bytes 786440 | tf_op jit(solution)/shard_map/ppermute | solution.py:35
  99.7 22.5 %collective-permute-start.26 = (bf16[8,128,128]{2,1,0:T(8,128)(2,1)S(1)}, bf16[8,128,128]{2,1,0:T(8,128)(2,1)S(1)}, u32[]{:S(2)}, u32[]{:S(2)}) collective-permute-start(bf16[8,128,128]{2,1,0:T(8,128)(2,1)S(1)} %fusion.5.pull), channel_id=1, source_target_pairs={{0,1},{1,0},{2,3},{3,2},{4,5},{5,4},{6,7},{7,6},{8,9},{9,8},{10,11... | collective-permute-start | bytes 786440 | tf_op jit(solution)/shard_map/ppermute | solution.py:35
  (15 other events, 99.7 us)

commit v3 on v2

--- a/solution.py
+++ b/solution.py
@@ -135,13 +135,15 @@
         for index in ids:
             lanes, here = lanes_of(start + index, dim), lanes_of(index, dim)
             states = [bucket[offset + index] for bucket, offset in buckets]
-            loads.append(
-                (query[:, lanes], cot[:, lanes], out_in[:, here], query_grad_in[:, here], codes[start + index], states)
-            )
+            loads.append((query[:, lanes], cot[:, lanes], out_in[:, here], query_grad_in[:, here], states))
+        _, rows, length = codes.shape
+        columns = codes[pl.ds(start + ids[0], len(ids))].astype(F32).reshape(len(ids) * rows, length).T
         results = []
-        for q, g, added, grad_added, code, states in loads:
-            columns = code.astype(F32).T
-            row_scales = [columns[:, first + b : first + b + 1] * (scales[b] * info[1 + b].astype(F32)) for b in levels]
+        for place, (q, g, added, grad_added, states) in enumerate(loads):
+            row_scales = []
+            for b in levels:
+                column = place * rows + first + b
+                row_scales.append(columns[:, column : column + 1] * (scales[b] * info[1 + b].astype(F32)))
             wide_q = jnp.concatenate([(q.astype(F32) * by).astype(BF16) for by in row_scales], axis=1)
             wide_g = jnp.concatenate([(g.astype(F32) * by).astype(BF16) for by in row_scales], axis=1)
             results.append(
@@ -201,6 +203,28 @@
             key_grad[:, here], value_grad[:, here] = left, right
 
     each(count, step, LAST_BATCH)
+
+
+def chosen_kernel(info, pull, grad, total, both, *, bit):
+    @pl.when(info[1 + bit] == 0)
+    def _():
+        both[...] = total[...]
+
+    @pl.when(info[1 + bit] != 0)
+    def _():
+        both[...] = plus(pull[...], grad[...])
+
+
+def taken_kernel(info, pull, total, swap, pull_out, total_out, *, bit):
+    @pl.when(info[1 + bit] == 0)
+    def _():
+        pull_out[...] = plus(pull[...], swap[...])
+
+    @pl.when(info[1 + bit] != 0)
+    def _():
+        pull_out[...] = pull[...]
+
+    total_out[...] = plus(total[...], swap[...])
 
 
 def flush_kernel(info, *refs, body, count, dim, groups):
@@ -299,28 +323,24 @@
         ((1, 0),) + tuple((0, half * at) for at in range(rest - 1)),
         ((1, half),) + tuple((1, half * (2 + at)) for at in range(rest - 1)),
     )
-    kept, sent = grad_states(tuple(range(rest)), table, [state_out(half * (rest - 1)), state_out(half * (rest + 1))])
+    kept, sent_grads = grad_states(
+        tuple(range(rest)), table, [state_out(half * (rest - 1)), state_out(half * (rest + 1))]
+    )
 
     near_own = exchanged(other, "head", 1)
     near_other = exchanged(own, "head", 1)
     top_partner = exchanged(top_other, "head", 1)
-    near_grads = exchanged(sent, "head", 1)
+    near_grads = exchanged(sent_grads, "head", 1)
 
     arrived = {}
     running = {}
     tops = {}
     for part in parts:
         running[part] = plus(piece(own, part * count), piece(near_own, part * count))
-    for at, (axis, mask) in enumerate(hops):
+    for at, (axis, mask) in enumerate(hops[:-1]):
         for part in parts:
-            sends = (lambda i: not i & step_bit) if at + 1 == len(hops) else None
-            arrived[at, part] = exchanged(running[part], axis, mask, sends)
+            arrived[at, part] = exchanged(running[part], axis, mask)
             running[part] = plus(running[part], arrived[at, part])
-    for part in parts:
-        over = exchanged(running[part], "ctx", last | step_bit, lambda i: not i & last and bool(i & step_bit))
-        relay = exchanged(over, "ctx", step_bit, lambda i: i & last and not i & step_bit)
-        tops[part] = plus(over, relay)
-        tops[part + CHUNKS] = exchanged(tops[part], "head", 1)
 
     pulled = {}
     for part in parts:
@@ -332,12 +352,28 @@
     pair_grads = lax.optimization_barrier(
         [plus(piece(kept, offset), piece(near_grads, 2 * half + offset)) for offset in offsets]
     )
-    for at in range(len(hops) - 1, -1, -1):
+
+    at = len(hops) - 1
+    axis, mask = hops[at]
+    bit = head_bits + ctx_bits - 2
+    for part in parts:
+        given = [info, pulled[part], pair_grads[at * CHUNKS + part], running[part]]
+        (both,) = run(functools.partial(chosen_kernel, bit=bit), given, [state_out(count)], 0.01)
+        arrived[at, part] = exchanged(both, axis, mask)
+        given = [info, pulled[part], running[part], arrived[at, part]]
+        pulled[part], running[part] = run(functools.partial(taken_kernel, bit=bit), given, [state_out(count)] * 2, 0.01)
+
+    for part in parts:
+        over = exchanged(running[part], "ctx", last | step_bit, lambda i: not i & last and bool(i & step_bit))
+        relay = exchanged(over, "ctx", step_bit, lambda i: i & last and not i & step_bit)
+        tops[part] = plus(over, relay)
+        tops[part + CHUNKS] = exchanged(tops[part], "head", 1)
+
+    for at in range(len(hops) - 2, -1, -1):
         axis, mask = hops[at]
         for part in parts:
-            grad = pair_grads[at * CHUNKS + part]
-            grad = plus(pulled[part], grad)
-            grad = exchanged(grad, axis, mask, (lambda i: i & step_bit) if at + 1 == len(hops) else None)
+            grad = plus(pulled[part], pair_grads[at * CHUNKS + part])
+            grad = exchanged(grad, axis, mask)
             pulled[part] = plus(pulled[part], grad)
     for part in parts:
         pulled[part + CHUNKS] = exchanged(pulled[part], "head", 1)

time: 125 us -> 110 us (0.88)
  waiting for transfers between devices: 59.7 us -> 40.4 us
  starting transfers between devices: 27 us -> 29.4 us
    ppermute x33 -> x31, waiting for transfers between devices: 59.7 us -> 40.4 us  [exchanged(): lax.ppermute(block, axis, [(index, index ^ mask) for index in indices if...]
    ppermute x33 -> x31, starting transfers between devices: 27 us -> 29.4 us  [exchanged(): lax.ppermute(block, axis, [(index, index ^ mask) for index in indices if...]
    unnamed x15 -> x17, local copies, waits for them, and re-layouts: 2.49 us -> 3.71 us
    pallas_call x19 -> x23, Pallas kernels: 29.9 us -> 30.6 us  [run(): pl.pallas_call(body, in_specs=[in_smem if arg is info else in_vmem for ar...]
    convert_element_type x21 -> x17, other arithmetic: 2.54 us -> 2.21 us  [plus(): return (left.astype(F32) + right.astype(F32)).astype(BF16)]
  transfers between devices with their start and end apart: 33 -> 31, of which waited for: 12 -> 12; matrix products, arithmetic and copies ran while one was open for 2% -> 2% of each run, Pallas kernels for 22% -> 24%
where the time goes in v3:
time: 110 us; the launch traced here: 109 us
  waiting for transfers between devices  40.4 us (37%)
  Pallas kernels  30.6 us (28%)
  starting transfers between devices  29.4 us (27%)
  local copies, waits for them, and re-layouts  3.84 us (3%)
  other arithmetic  3.39 us (3%)
  between operations  1.44 us (1%)
    ppermute x31, waiting for transfers between devices, exchanged(): lax.ppermute(block, axis, [(index, index ^ mask) for index in indices if...  40.4 us
    pallas_call x23, Pallas kernels, run(): pl.pallas_call(body, in_specs=[in_smem if arg is info else in_vmem for ar...  30.6 us
    ppermute x31, starting transfers between devices, exchanged(): lax.ppermute(block, axis, [(index, index ^ mask) for index in indices if...  29.4 us
    unnamed x17, local copies, waits for them, and re-layouts  3.71 us
    convert_element_type x17, other arithmetic, plus(): return (left.astype(F32) + right.astype(F32)).astype(BF16)  2.21 us
  transfers between devices with their start and end apart: 31, of which 12 were waited for; matrix products, arithmetic and copies ran while one was open for 2% of the time, Pallas kernels for 24%

profile of v3, /device:TPU:0, one launch (start us, length us, event | category | flops | bytes accessed | tf_op | source)
XLA Modules:
  0.0 109.1 jit_solution(17339935900235569628)
XLA Ops:
  1.7 2.5 %collective-permute-start = (bf16[8,16,128]{2,1,0:T(8,128)(2,1)S(1)}, bf16[8,16,128]{2,1,0:T(8,128)(2,1)S(1)}, u32[]{:S(2)}, u32[]{:S(2)}) collective-permute-start(bf16[8,16,128]{2,1,0:T(8,128)(2,1)S(1)} %bitcast.26), channel_id=1, source_target_pairs={{0,3},{1,2},{2,1},{3,0},{4,7},{5,6},{6,5},{7,4},{8,11},{9,10},{10,... | collective-permute-start | bytes 98312 | tf_op jit(solution)/shard_map/ppermute | solution.py:35
  6.0 2.2 %collective-permute-done.1 = bf16[8,16,128]{2,1,0:T(8,128)(2,1)S(1)} collective-permute-done((bf16[8,16,128]{2,1,0:T(8,128)(2,1)S(1)}, bf16[8,16,128]{2,1,0:T(8,128)(2,1)S(1)}, u32[]{:S(2)}, u32[]{:S(2)}) %collective-permute-start.1) | collective-permute-done | bytes 32800 | tf_op jit(solution)/shard_map/ppermute | solution.py:35
  10.7 2.5 %shard_map.87 = (bf16[48,128,128]{2,1,0:T(8,128)(2,1)S(1)}, bf16[80,128,128]{2,1,0:T(8,128)(2,1)S(1)}) custom-call(s32[6]{0:T(128)S(1)} %stack.24.info, bf16[128,4096]{1,0:T(8,128)(2,1)S(1)} %copy-done, bf16[128,4096]{1,0:T(8,128)(2,1)S(1)} %copy-done.2, bf16[32,16,128]{2,1,0:T(8,128)(2,1)S(1)} %pad_maximum_fusion.2.codes.refs_2_), custom_call_target="tpu_custom_call" | custom-call | flops 536870912 | tf_op jit(solution)/shard_map/pallas_call | solution.py:295
  22.7 5.6 %collective-permute-done.5.refs_1_ = bf16[8,128,128]{2,1,0:T(8,128)(2,1)S(1)} collective-permute-done((bf16[8,128,128]{2,1,0:T(8,128)(2,1)S(1)}, bf16[8,128,128]{2,1,0:T(8,128)(2,1)S(1)}, u32[]{:S(2)}, u32[]{:S(2)}) %collective-permute-start.5) | collective-permute-done | bytes 262176 | tf_op jit(solution)/shard_map/ppermute | solution.py:35
  28.4 1.6 %collective-permute-start.6 = (bf16[8,128,128]{2,1,0:T(8,128)(2,1)S(1)}, bf16[8,128,128]{2,1,0:T(8,128)(2,1)S(1)}, u32[]{:S(2)}, u32[]{:S(2)}) collective-permute-start(bf16[8,128,128]{2,1,0:T(8,128)(2,1)S(1)} %add_convert_fusion.16), channel_id=1, source_target_pairs={{0,4},{4,0},{8,12},{12,8},{16,20},{20,16},{24,28},{28,24},{1,5},{5... | collective-permute-start | bytes 786440 | tf_op jit(solution)/shard_map/ppermute | solution.py:35
  30.0 3.1 %collective-permute-done.16.refs_1_ = bf16[8,128,128]{2,1,0:T(8,128)(2,1)S(1)} collective-permute-done((bf16[8,128,128]{2,1,0:T(8,128)(2,1)S(1)}, bf16[8,128,128]{2,1,0:T(8,128)(2,1)S(1)}, u32[]{:S(2)}, u32[]{:S(2)}) %collective-permute-start.16) | collective-permute-done | bytes 262176 | tf_op jit(solution)/shard_map/ppermute | solution.py:35
  33.2 1.6 %collective-permute-start.17 = (bf16[8,128,128]{2,1,0:T(8,128)(2,1)S(1)}, bf16[8,128,128]{2,1,0:T(8,128)(2,1)S(1)}, u32[]{:S(2)}, u32[]{:S(2)}) collective-permute-start(bf16[8,128,128]{2,1,0:T(8,128)(2,1)S(1)} %add_convert_fusion.4), channel_id=1, source_target_pairs={{0,4},{4,0},{8,12},{12,8},{16,20},{20,16},{24,28},{28,24},{1,5},{5... | collective-permute-start | bytes 786440 | tf_op jit(solution)/shard_map/ppermute | solution.py:35
  36.4 4.3 %collective-permute-done.17.refs_2_ = bf16[8,128,128]{2,1,0:T(8,128)(2,1)S(1)} collective-permute-done((bf16[8,128,128]{2,1,0:T(8,128)(2,1)S(1)}, bf16[8,128,128]{2,1,0:T(8,128)(2,1)S(1)}, u32[]{:S(2)}, u32[]{:S(2)}) %collective-permute-start.17) | collective-permute-done | bytes 262176 | tf_op jit(solution)/shard_map/ppermute | solution.py:35
  42.2 6.0 %collective-permute-start.11 = (bf16[8,128,128]{2,1,0:T(8,128)(2,1)S(1)}, bf16[8,128,128]{2,1,0:T(8,128)(2,1)S(1)}, u32[]{:S(2)}, u32[]{:S(2)}) collective-permute-start(bf16[8,128,128]{2,1,0:T(8,128)(2,1)S(1)} %shard_map.88), channel_id=1, source_target_pairs={{0,8},{4,12},{8,0},{12,4},{16,24},{20,28},{24,16},{28,20},{1,9},{5... | collective-permute-start | bytes 786440 | tf_op jit(solution)/shard_map/ppermute | solution.py:35
  48.7 3.1 %collective-permute-start.20 = (bf16[8,128,128]{2,1,0:T(8,128)(2,1)S(1)}, bf16[8,128,128]{2,1,0:T(8,128)(2,1)S(1)}, u32[]{:S(2)}, u32[]{:S(2)}) collective-permute-start(bf16[8,128,128]{2,1,0:T(8,128)(2,1)S(1)} %shard_map.92), channel_id=1, source_target_pairs={{0,8},{4,12},{8,0},{12,4},{16,24},{20,28},{24,16},{28,20},{1,9},{5... | collective-permute-start | bytes 786440 | tf_op jit(solution)/shard_map/ppermute | solution.py:35
  51.8 2.4 %collective-permute-done.11.swap.refs_3_ = bf16[8,128,128]{2,1,0:T(8,128)(2,1)S(1)} collective-permute-done((bf16[8,128,128]{2,1,0:T(8,128)(2,1)S(1)}, bf16[8,128,128]{2,1,0:T(8,128)(2,1)S(1)}, u32[]{:S(2)}, u32[]{:S(2)}) %collective-permute-start.11) | collective-permute-done | bytes 262176 | tf_op jit(solution)/shard_map/ppermute | solution.py:35
  55.6 2.6 %collective-permute-done.20.refs_3_.swap = bf16[8,128,128]{2,1,0:T(8,128)(2,1)S(1)} collective-permute-done((bf16[8,128,128]{2,1,0:T(8,128)(2,1)S(1)}, bf16[8,128,128]{2,1,0:T(8,128)(2,1)S(1)}, u32[]{:S(2)}, u32[]{:S(2)}) %collective-permute-start.20) | collective-permute-done | bytes 262176 | tf_op jit(solution)/shard_map/ppermute | solution.py:35
  60.2 1.6 %collective-permute-start.28 = (bf16[8,128,128]{2,1,0:T(8,128)(2,1)S(1)}, bf16[8,128,128]{2,1,0:T(8,128)(2,1)S(1)}, u32[]{:S(2)}, u32[]{:S(2)}) collective-permute-start(bf16[8,128,128]{2,1,0:T(8,128)(2,1)S(1)} %fusion.4), channel_id=1, source_target_pairs={{0,4},{4,0},{8,12},{12,8},{16,20},{20,16},{24,28},{28,24},{1,5},{5... | collective-permute-start | bytes 786440 | tf_op jit(solution)/shard_map/ppermute | solution.py:35
  62.1 6.7 %collective-permute-done.25 = bf16[8,128,128]{2,1,0:T(8,128)(2,1)S(1)} collective-permute-done((bf16[8,128,128]{2,1,0:T(8,128)(2,1)S(1)}, bf16[8,128,128]{2,1,0:T(8,128)(2,1)S(1)}, u32[]{:S(2)}, u32[]{:S(2)}) %collective-permute-start.25) | collective-permute-done | bytes 262176 | tf_op jit(solution)/shard_map/ppermute | solution.py:35
  69.7 2.2 %collective-permute-done.28 = bf16[8,128,128]{2,1,0:T(8,128)(2,1)S(1)} collective-permute-done((bf16[8,128,128]{2,1,0:T(8,128)(2,1)S(1)}, bf16[8,128,128]{2,1,0:T(8,128)(2,1)S(1)}, u32[]{:S(2)}, u32[]{:S(2)}) %collective-permute-start.28) | collective-permute-done | bytes 262176 | tf_op jit(solution)/shard_map/ppermute | solution.py:35
  75.2 6.9 %collective-permute-done.29 = bf16[8,128,128]{2,1,0:T(8,128)(2,1)S(1)} collective-permute-done((bf16[8,128,128]{2,1,0:T(8,128)(2,1)S(1)}, bf16[8,128,128]{2,1,0:T(8,128)(2,1)S(1)}, u32[]{:S(2)}, u32[]{:S(2)}) %collective-permute-start.29) | collective-permute-done | bytes 262176 | tf_op jit(solution)/shard_map/ppermute | solution.py:35
  82.8 2.3 %collective-permute-done.26 = bf16[8,128,128]{2,1,0:T(8,128)(2,1)S(1)} collective-permute-done((bf16[8,128,128]{2,1,0:T(8,128)(2,1)S(1)}, bf16[8,128,128]{2,1,0:T(8,128)(2,1)S(1)}, u32[]{:S(2)}, u32[]{:S(2)}) %collective-permute-start.26) | collective-permute-done | bytes 262176 | tf_op jit(solution)/shard_map/ppermute | solution.py:35
  87.2 1.5 %shard_map.91 = (f32[128,1024]{1,0:T(8,128)S(1)}, f32[128,1024]{1,0:T(8,128)S(1)}, f32[128,1024]{1,0:T(8,128)S(1)}, f32[128,1024]{1,0:T(8,128)S(1)}) custom-call(s32[6]{0:T(128)S(1)} %stack.24.info, bf16[128,4096]{1,0:T(8,128)(2,1)S(1)} %copy-done.1, bf16[128,4096]{1,0:T(8,128)(2,1)S(1)} %copy-done.4, bf16[128,4096]{1,0:T(8,128)(2,1)S(1)} %copy-done.6, ...), custom_call_target="tpu_custom_call" | custom-call | flops 201326592 | tf_op jit(solution)/shard_map/pallas_call | solution.py:295
  91.5 1.7 %shard_map.93 = (f32[128,1024]{1,0:T(8,128)S(1)}, f32[128,1024]{1,0:T(8,128)S(1)}) custom-call(s32[6]{0:T(128)S(1)} %stack.24.info, bf16[128,4096]{1,0:T(8,128)(2,1)S(1)} %copy-done.1, bf16[128,4096]{1,0:T(8,128)(2,1)S(1)} %copy-done.3, bf16[32,16,128]{2,1,0:T(8,128)(2,1)S(1)} %pad_maximum_fusion.2.codes.refs_2_, f32[128,1024]{1,0:T(8,128)S(1)} %get-tuple-element.72.out_in, ...), custom_call_target="tpu_custom_call" | custom-call | flops 268435456 | tf_op jit(solution)/shard_map/pallas_call | solution.py:295
  93.2 1.7 %shard_map.100 = (f32[128,1024]{1,0:T(8,128)S(1)}, f32[128,1024]{1,0:T(8,128)S(1)}) custom-call(s32[6]{0:T(128)S(1)} %stack.24.info, bf16[128,4096]{1,0:T(8,128)(2,1)S(1)} %copy-done.1, bf16[128,4096]{1,0:T(8,128)(2,1)S(1)} %copy-done.3, bf16[32,16,128]{2,1,0:T(8,128)(2,1)S(1)} %pad_maximum_fusion.2.codes.refs_2_, f32[128,1024]{1,0:T(8,128)S(1)} %get-tuple-element.86.out_in, ...), custom_call_target="tpu_custom_call" | custom-call | flops 268435456 | tf_op jit(solution)/shard_map/pallas_call | solution.py:295
  99.0 1.7 %shard_map.97 = (f32[128,1024]{1,0:T(8,128)S(1)}, f32[128,1024]{1,0:T(8,128)S(1)}) custom-call(s32[6]{0:T(128)S(1)} %stack.24.info, bf16[128,4096]{1,0:T(8,128)(2,1)S(1)} %copy-done.1, bf16[128,4096]{1,0:T(8,128)(2,1)S(1)} %copy-done.3, bf16[32,16,128]{2,1,0:T(8,128)(2,1)S(1)} %pad_maximum_fusion.2.codes.refs_2_, f32[128,1024]{1,0:T(8,128)S(1)} %get-tuple-element.80.out_in, ...), custom_call_target="tpu_custom_call" | custom-call | flops 268435456 | tf_op jit(solution)/shard_map/pallas_call | solution.py:295
  102.7 1.7 %shard_map.89 = (f32[128,1024]{1,0:T(8,128)S(1)}, f32[128,1024]{1,0:T(8,128)S(1)}) custom-call(s32[6]{0:T(128)S(1)} %stack.24.info, bf16[128,4096]{1,0:T(8,128)(2,1)S(1)} %copy-done.1, bf16[128,4096]{1,0:T(8,128)(2,1)S(1)} %copy-done.3, bf16[32,16,128]{2,1,0:T(8,128)(2,1)S(1)} %pad_maximum_fusion.2.codes.refs_2_, f32[128,1024]{1,0:T(8,128)S(1)} %get-tuple-element.60.out_in, ...), custom_call_target="tpu_custom_call" | custom-call | flops 268435456 | tf_op jit(solution)/shard_map/pallas_call | solution.py:295
  104.4 2.3 %shard_map.102 = (bf16[128,4096]{1,0:T(8,128)(2,1)}, bf16[128,4096]{1,0:T(8,128)(2,1)}) custom-call(s32[6]{0:T(128)S(1)} %stack.24.info, bf16[128,4096]{1,0:T(8,128)(2,1)S(1)} %copy-done.1, bf16[128,4096]{1,0:T(8,128)(2,1)S(1)} %copy-done.3, bf16[32,16,128]{2,1,0:T(8,128)(2,1)S(1)} %pad_maximum_fusion.2.codes.refs_2_, ...), custom_call_target="tpu_custom_call" | custom-call | flops 67108864 | tf_op jit(solution)/shard_map/pallas_call | solution.py:295
  106.8 2.2 %shard_map.106 = (bf16[128,4096]{1,0:T(8,128)(2,1)}, bf16[128,4096]{1,0:T(8,128)(2,1)}) custom-call(s32[6]{0:T(128)S(1)} %stack.24.info, bf16[128,4096]{1,0:T(8,128)(2,1)S(1)} %copy-done.4, bf16[128,4096]{1,0:T(8,128)(2,1)S(1)} %copy-done.6, bf16[80,128,128]{2,1,0:T(8,128)(2,1)S(1)} %collective-permute-done.10.near.refs_2_, ...), custom_call_target="tpu_custom_call" | custom-call | flops 67108864 | tf_op jit(solution)/shard_map/pallas_call | solution.py:295
  (103 shorter events, 37.8 us)
Async XLA Ops:
  13.2 27.6 %collective-permute-start.10 = (bf16[80,128,128]{2,1,0:T(8,128)(2,1)S(1)}, bf16[80,128,128]{2,1,0:T(8,128)(2,1)S(1)}, u32[]{:S(2)}, u32[]{:S(2)}) collective-permute-start(bf16[80,128,128]{2,1,0:T(8,128)(2,1)S(1)} %get-tuple-element.67), channel_id=1, source_target_pairs={{0,1},{1,0},{2,3},{3,2},{4,5},{5,4},{6,7},{7,6},{8,9},{9,8},{10,11... | collective-permute-start | bytes 7864328 | tf_op jit(solution)/shard_map/ppermute | solution.py:35
  19.1 9.2 %collective-permute-start.5 = (bf16[8,128,128]{2,1,0:T(8,128)(2,1)S(1)}, bf16[8,128,128]{2,1,0:T(8,128)(2,1)S(1)}, u32[]{:S(2)}, u32[]{:S(2)}) collective-permute-start(bf16[8,128,128]{2,1,0:T(8,128)(2,1)S(1)} %get-tuple-element.125), channel_id=1, source_target_pairs={{0,2},{1,3},{2,0},{3,1},{4,6},{5,7},{6,4},{7,5},{8,10},{9,11},{10,... | collective-permute-start | bytes 786440 | tf_op jit(solution)/shard_map/ppermute | solution.py:35
  20.1 13.0 %collective-permute-start.16 = (bf16[8,128,128]{2,1,0:T(8,128)(2,1)S(1)}, bf16[8,128,128]{2,1,0:T(8,128)(2,1)S(1)}, u32[]{:S(2)}, u32[]{:S(2)}) collective-permute-start(bf16[8,128,128]{2,1,0:T(8,128)(2,1)S(1)} %get-tuple-element.124), channel_id=1, source_target_pairs={{0,2},{1,3},{2,0},{3,1},{4,6},{5,7},{6,4},{7,5},{8,10},{9,11},{10,... | collective-permute-start | bytes 786440 | tf_op jit(solution)/shard_map/ppermute | solution.py:35
  21.3 13.4 %collective-permute-start.8 = (bf16[8,128,128]{2,1,0:T(8,128)(2,1)S(1)}, bf16[8,128,128]{2,1,0:T(8,128)(2,1)S(1)}, u32[]{:S(2)}, u32[]{:S(2)}) collective-permute-start(bf16[8,128,128]{2,1,0:T(8,128)(2,1)S(1)} %get-tuple-element.123), channel_id=1, source_target_pairs={{24,16},{28,20},{25,17},{29,21},{26,18},{30,22},{27,19},{31,23}} | collective-permute-start | bytes 786440 | tf_op jit(solution)/shard_map/ppermute | solution.py:35
  22.0 13.5 %collective-permute-start.18 = (bf16[8,128,128]{2,1,0:T(8,128)(2,1)S(1)}, bf16[8,128,128]{2,1,0:T(8,128)(2,1)S(1)}, u32[]{:S(2)}, u32[]{:S(2)}) collective-permute-start(bf16[8,128,128]{2,1,0:T(8,128)(2,1)S(1)} %get-tuple-element.122), channel_id=1, source_target_pairs={{24,16},{28,20},{25,17},{29,21},{26,18},{30,22},{27,19},{31,23}} | collective-permute-start | bytes 786440 | tf_op jit(solution)/shard_map/ppermute | solution.py:35
  28.4 7.9 %collective-permute-start.6 = (bf16[8,128,128]{2,1,0:T(8,128)(2,1)S(1)}, bf16[8,128,128]{2,1,0:T(8,128)(2,1)S(1)}, u32[]{:S(2)}, u32[]{:S(2)}) collective-permute-start(bf16[8,128,128]{2,1,0:T(8,128)(2,1)S(1)} %add_convert_fusion.16), channel_id=1, source_target_pairs={{0,4},{4,0},{8,12},{12,8},{16,20},{20,16},{24,28},{28,24},{1,5},{5... | collective-permute-start | bytes 786440 | tf_op jit(solution)/shard_map/ppermute | solution.py:35
  33.2 7.6 %collective-permute-start.17 = (bf16[8,128,128]{2,1,0:T(8,128)(2,1)S(1)}, bf16[8,128,128]{2,1,0:T(8,128)(2,1)S(1)}, u32[]{:S(2)}, u32[]{:S(2)}) collective-permute-start(bf16[8,128,128]{2,1,0:T(8,128)(2,1)S(1)} %add_convert_fusion.4), channel_id=1, source_target_pairs={{0,4},{4,0},{8,12},{12,8},{16,20},{20,16},{24,28},{28,24},{1,5},{5... | collective-permute-start | bytes 786440 | tf_op jit(solution)/shard_map/ppermute | solution.py:35
  34.8 6.8 %collective-permute-start.9 = (bf16[8,128,128]{2,1,0:T(8,128)(2,1)S(1)}, bf16[8,128,128]{2,1,0:T(8,128)(2,1)S(1)}, u32[]{:S(2)}, u32[]{:S(2)}) collective-permute-start(bf16[8,128,128]{2,1,0:T(8,128)(2,1)S(1)} %add_convert_fusion.14), channel_id=1, source_target_pairs={{16,8},{20,12},{17,9},{21,13},{18,10},{22,14},{19,11},{23,15}} | collective-permute-start | bytes 786440 | tf_op jit(solution)/shard_map/ppermute | solution.py:35
  35.6 12.6 %collective-permute-start.19 = (bf16[8,128,128]{2,1,0:T(8,128)(2,1)S(1)}, bf16[8,128,128]{2,1,0:T(8,128)(2,1)S(1)}, u32[]{:S(2)}, u32[]{:S(2)}) collective-permute-start(bf16[8,128,128]{2,1,0:T(8,128)(2,1)S(1)} %add_convert_fusion.2), channel_id=1, source_target_pairs={{16,8},{20,12},{17,9},{21,13},{18,10},{22,14},{19,11},{23,15}} | collective-permute-start | bytes 786440 | tf_op jit(solution)/shard_map/ppermute | solution.py:35
  42.2 12.0 %collective-permute-start.11 = (bf16[8,128,128]{2,1,0:T(8,128)(2,1)S(1)}, bf16[8,128,128]{2,1,0:T(8,128)(2,1)S(1)}, u32[]{:S(2)}, u32[]{:S(2)}) collective-permute-start(bf16[8,128,128]{2,1,0:T(8,128)(2,1)S(1)} %shard_map.88), channel_id=1, source_target_pairs={{0,8},{4,12},{8,0},{12,4},{16,24},{20,28},{24,16},{28,20},{1,9},{5... | collective-permute-start | bytes 786440 | tf_op jit(solution)/shard_map/ppermute | solution.py:35
  48.7 9.4 %collective-permute-start.20 = (bf16[8,128,128]{2,1,0:T(8,128)(2,1)S(1)}, bf16[8,128,128]{2,1,0:T(8,128)(2,1)S(1)}, u32[]{:S(2)}, u32[]{:S(2)}) collective-permute-start(bf16[8,128,128]{2,1,0:T(8,128)(2,1)S(1)} %shard_map.92), channel_id=1, source_target_pairs={{0,8},{4,12},{8,0},{12,4},{16,24},{20,28},{24,16},{28,20},{1,9},{5... | collective-permute-start | bytes 786440 | tf_op jit(solution)/shard_map/ppermute | solution.py:35
  51.8 30.4 %collective-permute-start.3 = (bf16[16,128,128]{2,1,0:T(8,128)(2,1)S(1)}, bf16[16,128,128]{2,1,0:T(8,128)(2,1)S(1)}, u32[]{:S(2)}, u32[]{:S(2)}) collective-permute-start(bf16[16,128,128]{2,1,0:T(8,128)(2,1)S(1)} %get-tuple-element.62), channel_id=1, source_target_pairs={{0,1},{1,0},{2,3},{3,2},{4,5},{5,4},{6,7},{7,6},{8,9},{9,8},{10,11... | collective-permute-start | bytes 1572872 | tf_op jit(solution)/shard_map/ppermute | solution.py:35
  54.9 7.1 %collective-permute-start.13 = (bf16[8,128,128]{2,1,0:T(8,128)(2,1)S(1)}, bf16[8,128,128]{2,1,0:T(8,128)(2,1)S(1)}, u32[]{:S(2)}, u32[]{:S(2)}) collective-permute-start(bf16[8,128,128]{2,1,0:T(8,128)(2,1)S(1)} %get-tuple-element.71), channel_id=1, source_target_pairs={{8,16},{12,20},{9,17},{13,21},{10,18},{14,22},{11,19},{15,23}} | collective-permute-start | bytes 786440 | tf_op jit(solution)/shard_map/ppermute | solution.py:35
  58.8 10.8 %collective-permute-start.21 = (bf16[8,128,128]{2,1,0:T(8,128)(2,1)S(1)}, bf16[8,128,128]{2,1,0:T(8,128)(2,1)S(1)}, u32[]{:S(2)}, u32[]{:S(2)}) collective-permute-start(bf16[8,128,128]{2,1,0:T(8,128)(2,1)S(1)} %get-tuple-element.77), channel_id=1, source_target_pairs={{8,16},{12,20},{9,17},{13,21},{10,18},{14,22},{11,19},{15,23}} | collective-permute-start | bytes 786440 | tf_op jit(solution)/shard_map/ppermute | solution.py:35
  59.6 9.2 %collective-permute-start.25 = (bf16[8,128,128]{2,1,0:T(8,128)(2,1)S(1)}, bf16[8,128,128]{2,1,0:T(8,128)(2,1)S(1)}, u32[]{:S(2)}, u32[]{:S(2)}) collective-permute-start(bf16[8,128,128]{2,1,0:T(8,128)(2,1)S(1)} %fusion), channel_id=1, source_target_pairs={{0,4},{4,0},{8,12},{12,8},{16,20},{20,16},{24,28},{28,24},{1,5},{5... | collective-permute-start | bytes 786440 | tf_op jit(solution)/shard_map/ppermute | solution.py:35
  60.2 11.7 %collective-permute-start.28 = (bf16[8,128,128]{2,1,0:T(8,128)(2,1)S(1)}, bf16[8,128,128]{2,1,0:T(8,128)(2,1)S(1)}, u32[]{:S(2)}, u32[]{:S(2)}) collective-permute-start(bf16[8,128,128]{2,1,0:T(8,128)(2,1)S(1)} %fusion.4), channel_id=1, source_target_pairs={{0,4},{4,0},{8,12},{12,8},{16,20},{20,16},{24,28},{28,24},{1,5},{5... | collective-permute-start | bytes 786440 | tf_op jit(solution)/shard_map/ppermute | solution.py:35
  62.0 40.7 %collective-permute-start.12 = (bf16[24,128,128]{2,1,0:T(8,128)(2,1)S(1)}, bf16[24,128,128]{2,1,0:T(8,128)(2,1)S(1)}, u32[]{:S(2)}, u32[]{:S(2)}) collective-permute-start(bf16[24,128,128]{2,1,0:T(8,128)(2,1)S(1)} %pad_maximum_fusion), channel_id=1, source_target_pairs={{0,1},{1,0},{2,3},{3,2},{4,5},{5,4},{6,7},{7,6},{8,9},{9,8},{10,11... | collective-permute-start | bytes 2359304 | tf_op jit(solution)/shard_map/ppermute | solution.py:35
  69.6 15.6 %collective-permute-start.23 = (bf16[24,128,128]{2,1,0:T(8,128)(2,1)S(1)}, bf16[24,128,128]{2,1,0:T(8,128)(2,1)S(1)}, u32[]{:S(2)}, u32[]{:S(2)}) collective-permute-start(bf16[24,128,128]{2,1,0:T(8,128)(2,1)S(1)} %pad_maximum_fusion.1), channel_id=1, source_target_pairs={{0,1},{1,0},{2,3},{3,2},{4,5},{5,4},{6,7},{7,6},{8,9},{9,8},{10,11... | collective-permute-start | bytes 2359304 | tf_op jit(solution)/shard_map/ppermute | solution.py:35
  72.9 9.2 %collective-permute-start.29 = (bf16[8,128,128]{2,1,0:T(8,128)(2,1)S(1)}, bf16[8,128,128]{2,1,0:T(8,128)(2,1)S(1)}, u32[]{:S(2)}, u32[]{:S(2)}) collective-permute-start(bf16[8,128,128]{2,1,0:T(8,128)(2,1)S(1)} %fusion.6), channel_id=1, source_target_pairs={{0,2},{1,3},{2,0},{3,1},{4,6},{5,7},{6,4},{7,5},{8,10},{9,11},{10,... | collective-permute-start | bytes 786440 | tf_op jit(solution)/shard_map/ppermute | solution.py:35
  74.0 11.1 %collective-permute-start.26 = (bf16[8,128,128]{2,1,0:T(8,128)(2,1)S(1)}, bf16[8,128,128]{2,1,0:T(8,128)(2,1)S(1)}, u32[]{:S(2)}, u32[]{:S(2)}) collective-permute-start(bf16[8,128,128]{2,1,0:T(8,128)(2,1)S(1)} %fusion.2), channel_id=1, source_target_pairs={{0,2},{1,3},{2,0},{3,1},{4,6},{5,7},{6,4},{7,5},{8,10},{9,11},{10,... | collective-permute-start | bytes 786440 | tf_op jit(solution)/shard_map/ppermute | solution.py:35
  82.1 22.3 %collective-permute-start.15 = (bf16[8,128,128]{2,1,0:T(8,128)(2,1)S(1)}, bf16[8,128,128]{2,1,0:T(8,128)(2,1)S(1)}, u32[]{:S(2)}, u32[]{:S(2)}) collective-permute-start(bf16[8,128,128]{2,1,0:T(8,128)(2,1)S(1)} %add_convert_fusion.6.bucket), channel_id=1, source_target_pairs={{0,1},{1,0},{2,3},{3,2},{4,5},{5,4},{6,7},{7,6},{8,9},{9,8},{10,11... | collective-permute-start | bytes 786440 | tf_op jit(solution)/shard_map/ppermute | solution.py:35
  82.2 18.4 %collective-permute-start.24 = (bf16[8,128,128]{2,1,0:T(8,128)(2,1)S(1)}, bf16[8,128,128]{2,1,0:T(8,128)(2,1)S(1)}, u32[]{:S(2)}, u32[]{:S(2)}) collective-permute-start(bf16[8,128,128]{2,1,0:T(8,128)(2,1)S(1)} %add_convert_fusion.bucket), channel_id=1, source_target_pairs={{0,1},{1,0},{2,3},{3,2},{4,5},{5,4},{6,7},{7,6},{8,9},{9,8},{10,11... | collective-permute-start | bytes 786440 | tf_op jit(solution)/shard_map/ppermute | solution.py:35
  85.1 16.7 %collective-permute-start.30 = (bf16[8,128,128]{2,1,0:T(8,128)(2,1)S(1)}, bf16[8,128,128]{2,1,0:T(8,128)(2,1)S(1)}, u32[]{:S(2)}, u32[]{:S(2)}) collective-permute-start(bf16[8,128,128]{2,1,0:T(8,128)(2,1)S(1)} %fusion.7.pull), channel_id=1, source_target_pairs={{0,1},{1,0},{2,3},{3,2},{4,5},{5,4},{6,7},{7,6},{8,9},{9,8},{10,11... | collective-permute-start | bytes 786440 | tf_op jit(solution)/shard_map/ppermute | solution.py:35
  85.2 21.5 %collective-permute-start.27 = (bf16[8,128,128]{2,1,0:T(8,128)(2,1)S(1)}, bf16[8,128,128]{2,1,0:T(8,128)(2,1)S(1)}, u32[]{:S(2)}, u32[]{:S(2)}) collective-permute-start(bf16[8,128,128]{2,1,0:T(8,128)(2,1)S(1)} %fusion.3.pull), channel_id=1, source_target_pairs={{0,1},{1,0},{2,3},{3,2},{4,5},{5,4},{6,7},{7,6},{8,9},{9,8},{10,11... | collective-permute-start | bytes 786440 | tf_op jit(solution)/shard_map/ppermute | solution.py:35
  (14 other events, 67.1 us)
